TPU v7x, 32 devices: a 4x4x1 block of a 4x4x8 slice. The times are simulated.
32 devices in a mesh: dp: 1 (over z), row: 4 (over y), col: 8 (over x, core).
Axes of the slice: x: 4, y: 4, z: 1, core: 2. Of those that a mesh axis runs over, the one named last changes fastest.
The devices are a block of a 4x4x8 slice.
Arguments:
- pair_rep: bfloat16 [1024, 1024, 128], P(('dp', 'row'), 'col')
- res_mask: int32 [1024], P('dp')
- ln_gamma: float32 [128], replicated
- ln_beta: float32 [128], replicated
- w_q: bfloat16 [128, 128], replicated
- w_k: bfloat16 [128, 128], replicated
- w_v: bfloat16 [128, 128], replicated
- w_g: bfloat16 [128, 128], replicated
- w_b: bfloat16 [128, 4], replicated
- w_o: bfloat16 [128, 128], replicated
Outputs:
- output: bfloat16 [1024, 1024, 128], P(('dp', 'row'), 'col')
All inputs are finite; a program needn't handle non-finite values.
Results may differ from a plain program's by a relative error of at most 0.00680541.
Values are sent between devices in bfloat16 or wider.
A program may use at most 768 MiB of HBM per device.

v0:
```python
import jax
import jax.numpy as jnp
from jax import lax
from jax.sharding import PartitionSpec as P

LN_EPS = 1e-5
MASK_NEG = -1e9


def layer_norm(z_rows, ln_gamma, ln_beta):
    z_float = z_rows.astype(jnp.float32)
    row_mean = jnp.mean(z_float, axis=-1, keepdims=True)
    centered = z_float - row_mean
    row_var = jnp.mean(centered * centered, axis=-1, keepdims=True)
    normed = centered * lax.rsqrt(row_var + LN_EPS) * ln_gamma + ln_beta
    return normed.astype(jnp.bfloat16)


def local_heads(normed, weight, factor, n_heads):
    projected = jnp.einsum("ijc,cn->ijn", normed, weight, preferred_element_type=jnp.float32) * factor
    n_rows_loc, n_cols_loc, width = projected.shape
    return projected.astype(jnp.bfloat16).reshape(n_rows_loc, n_cols_loc, n_heads, width // n_heads)


def row_group_size(n_rows_loc, n_keys, pair_dim, n_heads):
    row_limit = max(1, (n_rows_loc * pair_dim) // (2 * n_keys * n_heads))
    return max(group_size for group_size in range(1, n_rows_loc + 1) if n_rows_loc % group_size == 0 and group_size <= row_limit)


def fold_keys(q_groups, k_groups, v_groups, blk_bias, soft_state):
    max_all, sum_all, acc_all = soft_state

    def one_group(group_args):
        q_rows, k_rows, v_rows, max_old, sum_old, acc_old = group_args
        logits = jnp.einsum("ijhd,ikhd->ihjk", q_rows, k_rows, preferred_element_type=jnp.float32) + blk_bias
        max_new = jnp.maximum(max_old, jnp.max(logits, axis=-1))
        correction = jnp.exp(max_old - max_new)
        att_weight = jnp.exp(logits - max_new[..., None])
        sum_new = sum_old * correction + jnp.sum(att_weight, axis=-1)
        acc_new = acc_old * correction[..., None] + jnp.einsum("ihjk,ikhd->ihjd", att_weight.astype(jnp.bfloat16), v_rows, preferred_element_type=jnp.float32)
        return max_new, sum_new, acc_new

    return lax.map(one_group, (q_groups, k_groups, v_groups, max_all, sum_all, acc_all))


def solution(mesh):
    n_cols = mesh.shape["col"]
    tile_spec = P(("dp", "row"), "col", None)
    replicated = P()
    shift_pairs = [(src_dev, (src_dev - 1) % n_cols) for src_dev in range(n_cols)]

    def local_fn(z_tile, res_mask, ln_gamma, ln_beta, w_q, w_k, w_v, w_g, w_b, w_o):
        n_rows_loc, n_keys, pair_dim = z_tile.shape
        n_heads = w_b.shape[1]
        head_dim = w_q.shape[1] // n_heads
        col_index = lax.axis_index("col")
        normed = layer_norm(z_tile, ln_gamma, ln_beta)
        q_tile = local_heads(normed, w_q, head_dim ** -0.5, n_heads)
        k_tile = local_heads(normed, w_k, 1.0, n_heads)
        v_tile = local_heads(normed, w_v, 1.0, n_heads)
        gate_vals = jax.nn.sigmoid(jnp.einsum("ijc,chd->ihjd", normed, w_g.reshape(pair_dim, n_heads, head_dim), preferred_element_type=jnp.float32))
        bias_tile = jnp.einsum("jkc,ch->hjk", normed, w_b, preferred_element_type=jnp.float32).astype(jnp.bfloat16)
        bias_cols = lax.all_gather(bias_tile, "row", axis=1, tiled=True)
        bias_strip = lax.all_to_all(bias_cols, "col", 1, 2, tiled=True)
        key_add = jnp.where(res_mask > 0, 0.0, MASK_NEG).astype(jnp.float32)

        row_group = row_group_size(n_rows_loc, n_keys, pair_dim, n_heads)
        n_groups = n_rows_loc // row_group
        group_shape = (n_groups, row_group, n_keys, n_heads, head_dim)
        q_groups = q_tile.reshape(group_shape)
        state_shape = (n_groups, row_group, n_heads, n_keys)
        soft_state = (
            jnp.full(state_shape, -jnp.inf, jnp.float32),
            jnp.zeros(state_shape, jnp.float32),
            jnp.zeros(state_shape + (head_dim,), jnp.float32),
        )

        def fold_block(src_col, k_blk, v_blk, soft_state):
            key_start = src_col * n_keys
            blk_bias = lax.dynamic_slice_in_dim(bias_strip, key_start, n_keys, axis=2).astype(jnp.float32)
            blk_bias = blk_bias + lax.dynamic_slice_in_dim(key_add, key_start, n_keys)
            return fold_keys(q_groups, k_blk.reshape(group_shape), v_blk.reshape(group_shape), blk_bias, soft_state)

        soft_state = fold_block(col_index, k_tile, v_tile, soft_state)

        def col_step(step_idx, loop_carry):
            k_blk, v_blk, soft_state = loop_carry
            k_blk = lax.ppermute(k_blk, "col", shift_pairs)
            v_blk = lax.ppermute(v_blk, "col", shift_pairs)
            soft_state = fold_block((col_index + step_idx) % n_cols, k_blk, v_blk, soft_state)
            return k_blk, v_blk, soft_state

        loop_out = lax.fori_loop(1, n_cols, col_step, (k_tile, v_tile, soft_state))
        run_max, run_sum, run_acc = loop_out[2]
        attended = (run_acc / run_sum[..., None]).reshape(n_rows_loc, n_heads, n_keys, head_dim)
        gated_out = (gate_vals * attended).astype(jnp.bfloat16)
        update = jnp.einsum("ihjd,hdc->ijc", gated_out, w_o.reshape(n_heads, head_dim, pair_dim), preferred_element_type=jnp.float32)
        return (z_tile.astype(jnp.float32) + update).astype(jnp.bfloat16)

    return jax.shard_map(
        local_fn,
        mesh=mesh,
        in_specs=(tile_spec, P("dp"), replicated, replicated, replicated, replicated, replicated, replicated, replicated, replicated),
        out_specs=tile_spec,
        check_vma=False,
    )
```

profile of v0, /device:TPU:97, one launch (start us, length us, event | category | flops | bytes accessed | tf_op | source)
XLA Modules:
  0.0 2289.5 jit_solution(7497981254951944561)
XLA Ops:
  86.0 78.2 %while.72 = (s32[]{:T(128)}, f32[8,32,4,128]{3,2,1,0:T(4,128)S(1)}, f32[8,32,4,128]{3,2,1,0:T(4,128)S(1)}, f32[8,32,4,128,32]{3,4,2,1,0:T(8,128)}, bf16[8,32,128...) while((s32[]{:T(128)}, f32[8,32,4,128]{3,2,1,0:T(4,128)S(1)}, ...), condition=%wide.region_5.6_spmd, body=%wide.region_2.5_spmd.sunk | while | flops 285786112 | bytes 31918176 | solution.py:43
  164.2 2083.5 %while.74 = (s32[]{:T(128)}, bf16[256,128,4,32]{1,3,2,0:T(8,128)(2,1)}, bf16[256,128,4,32]{1,3,2,0:T(8,128)(2,1)}, f32[8,32,4,128]{3,2,1,0:T(4,128)S(1)}, f32[8,...) while((s32[]{:T(128)}, ...), condition=%wide.region_11.12_spmd, body=%wide.region_6.11_spmd.sunk | while | flops 286457888 | bytes 139530320 | solution.py:93
  167.6 89.7 %collective-permute-done = bf16[256,128,4,32]{1,3,2,0:T(8,128)(2,1)} collective-permute-done((bf16[256,128,4,32]{1,3,2,0:T(8,128)(2,1)}, bf16[256,128,4,32]{1,3,2,0:T(8,128)(2,1)}, u32[]{:S(2)}, u32[]{:S(2)}) %collective-permute-start) | collective-permute-done | bytes 8388640 | tf_op jit(solution)/shard_map/while/body/eval_jaxpr/ppermute | solution.py:88
  257.4 89.9 %collective-permute-done.1 = bf16[256,128,4,32]{1,3,2,0:T(8,128)(2,1)} collective-permute-done((bf16[256,128,4,32]{1,3,2,0:T(8,128)(2,1)}, bf16[256,128,4,32]{1,3,2,0:T(8,128)(2,1)}, u32[]{:S(2)}, u32[]{:S(2)}) %collective-permute-start.1) | collective-permute-done | bytes 8388640 | tf_op jit(solution)/shard_map/while/body/eval_jaxpr/ppermute | solution.py:89
  347.2 94.2 %while.75 = (s32[]{:T(128)}, f32[8,32,4,128]{3,2,1,0:T(4,128)S(1)}, f32[8,32,4,128]{3,2,1,0:T(4,128)S(1)}, f32[8,32,4,128,32]{3,4,2,1,0:T(8,128)}, bf16[8,32,128...) while((s32[]{:T(128)}, f32[8,32,4,128]{3,2,1,0:T(4,128)S(1)}, ...), condition=%wide.region_10.10_spmd.clone, body=%wide.region_7.9_spmd.clone.sunk | while | flops 286326784 | bytes 38471784 | solution.py:43
  466.4 88.5 %collective-permute-done = bf16[256,128,4,32]{1,3,2,0:T(8,128)(2,1)} collective-permute-done((bf16[256,128,4,32]{1,3,2,0:T(8,128)(2,1)}, bf16[256,128,4,32]{1,3,2,0:T(8,128)(2,1)}, u32[]{:S(2)}, u32[]{:S(2)}) %collective-permute-start) | collective-permute-done | bytes 8388640 | tf_op jit(solution)/shard_map/while/body/eval_jaxpr/ppermute | solution.py:88
  555.0 89.9 %collective-permute-done.1 = bf16[256,128,4,32]{1,3,2,0:T(8,128)(2,1)} collective-permute-done((bf16[256,128,4,32]{1,3,2,0:T(8,128)(2,1)}, bf16[256,128,4,32]{1,3,2,0:T(8,128)(2,1)}, u32[]{:S(2)}, u32[]{:S(2)}) %collective-permute-start.1) | collective-permute-done | bytes 8388640 | tf_op jit(solution)/shard_map/while/body/eval_jaxpr/ppermute | solution.py:89
  644.9 94.1 %while.75 = (s32[]{:T(128)}, f32[8,32,4,128]{3,2,1,0:T(4,128)S(1)}, f32[8,32,4,128]{3,2,1,0:T(4,128)S(1)}, f32[8,32,4,128,32]{3,4,2,1,0:T(8,128)}, bf16[8,32,128...) while((s32[]{:T(128)}, f32[8,32,4,128]{3,2,1,0:T(4,128)S(1)}, ...), condition=%wide.region_10.10_spmd.clone, body=%wide.region_7.9_spmd.clone.sunk | while | flops 286326784 | bytes 38471784 | solution.py:43
  765.3 87.3 %collective-permute-done = bf16[256,128,4,32]{1,3,2,0:T(8,128)(2,1)} collective-permute-done((bf16[256,128,4,32]{1,3,2,0:T(8,128)(2,1)}, bf16[256,128,4,32]{1,3,2,0:T(8,128)(2,1)}, u32[]{:S(2)}, u32[]{:S(2)}) %collective-permute-start) | collective-permute-done | bytes 8388640 | tf_op jit(solution)/shard_map/while/body/eval_jaxpr/ppermute | solution.py:88
  852.6 89.9 %collective-permute-done.1 = bf16[256,128,4,32]{1,3,2,0:T(8,128)(2,1)} collective-permute-done((bf16[256,128,4,32]{1,3,2,0:T(8,128)(2,1)}, bf16[256,128,4,32]{1,3,2,0:T(8,128)(2,1)}, u32[]{:S(2)}, u32[]{:S(2)}) %collective-permute-start.1) | collective-permute-done | bytes 8388640 | tf_op jit(solution)/shard_map/while/body/eval_jaxpr/ppermute | solution.py:89
  942.5 94.1 %while.75 = (s32[]{:T(128)}, f32[8,32,4,128]{3,2,1,0:T(4,128)S(1)}, f32[8,32,4,128]{3,2,1,0:T(4,128)S(1)}, f32[8,32,4,128,32]{3,4,2,1,0:T(8,128)}, bf16[8,32,128...) while((s32[]{:T(128)}, f32[8,32,4,128]{3,2,1,0:T(4,128)S(1)}, ...), condition=%wide.region_10.10_spmd.clone, body=%wide.region_7.9_spmd.clone.sunk | while | flops 286326784 | bytes 38471784 | solution.py:43
  1064.1 86.1 %collective-permute-done = bf16[256,128,4,32]{1,3,2,0:T(8,128)(2,1)} collective-permute-done((bf16[256,128,4,32]{1,3,2,0:T(8,128)(2,1)}, bf16[256,128,4,32]{1,3,2,0:T(8,128)(2,1)}, u32[]{:S(2)}, u32[]{:S(2)}) %collective-permute-start) | collective-permute-done | bytes 8388640 | tf_op jit(solution)/shard_map/while/body/eval_jaxpr/ppermute | solution.py:88
  1150.2 89.9 %collective-permute-done.1 = bf16[256,128,4,32]{1,3,2,0:T(8,128)(2,1)} collective-permute-done((bf16[256,128,4,32]{1,3,2,0:T(8,128)(2,1)}, bf16[256,128,4,32]{1,3,2,0:T(8,128)(2,1)}, u32[]{:S(2)}, u32[]{:S(2)}) %collective-permute-start.1) | collective-permute-done | bytes 8388640 | tf_op jit(solution)/shard_map/while/body/eval_jaxpr/ppermute | solution.py:89
  1240.1 94.1 %while.75 = (s32[]{:T(128)}, f32[8,32,4,128]{3,2,1,0:T(4,128)S(1)}, f32[8,32,4,128]{3,2,1,0:T(4,128)S(1)}, f32[8,32,4,128,32]{3,4,2,1,0:T(8,128)}, bf16[8,32,128...) while((s32[]{:T(128)}, f32[8,32,4,128]{3,2,1,0:T(4,128)S(1)}, ...), condition=%wide.region_10.10_spmd.clone, body=%wide.region_7.9_spmd.clone.sunk | while | flops 286326784 | bytes 38471784 | solution.py:43
  1362.9 84.9 %collective-permute-done = bf16[256,128,4,32]{1,3,2,0:T(8,128)(2,1)} collective-permute-done((bf16[256,128,4,32]{1,3,2,0:T(8,128)(2,1)}, bf16[256,128,4,32]{1,3,2,0:T(8,128)(2,1)}, u32[]{:S(2)}, u32[]{:S(2)}) %collective-permute-start) | collective-permute-done | bytes 8388640 | tf_op jit(solution)/shard_map/while/body/eval_jaxpr/ppermute | solution.py:88
  1447.8 89.9 %collective-permute-done.1 = bf16[256,128,4,32]{1,3,2,0:T(8,128)(2,1)} collective-permute-done((bf16[256,128,4,32]{1,3,2,0:T(8,128)(2,1)}, bf16[256,128,4,32]{1,3,2,0:T(8,128)(2,1)}, u32[]{:S(2)}, u32[]{:S(2)}) %collective-permute-start.1) | collective-permute-done | bytes 8388640 | tf_op jit(solution)/shard_map/while/body/eval_jaxpr/ppermute | solution.py:89
  1537.7 94.1 %while.75 = (s32[]{:T(128)}, f32[8,32,4,128]{3,2,1,0:T(4,128)S(1)}, f32[8,32,4,128]{3,2,1,0:T(4,128)S(1)}, f32[8,32,4,128,32]{3,4,2,1,0:T(8,128)}, bf16[8,32,128...) while((s32[]{:T(128)}, f32[8,32,4,128]{3,2,1,0:T(4,128)S(1)}, ...), condition=%wide.region_10.10_spmd.clone, body=%wide.region_7.9_spmd.clone.sunk | while | flops 286326784 | bytes 38471784 | solution.py:43
  1661.7 83.7 %collective-permute-done = bf16[256,128,4,32]{1,3,2,0:T(8,128)(2,1)} collective-permute-done((bf16[256,128,4,32]{1,3,2,0:T(8,128)(2,1)}, bf16[256,128,4,32]{1,3,2,0:T(8,128)(2,1)}, u32[]{:S(2)}, u32[]{:S(2)}) %collective-permute-start) | collective-permute-done | bytes 8388640 | tf_op jit(solution)/shard_map/while/body/eval_jaxpr/ppermute | solution.py:88
  1745.4 89.9 %collective-permute-done.1 = bf16[256,128,4,32]{1,3,2,0:T(8,128)(2,1)} collective-permute-done((bf16[256,128,4,32]{1,3,2,0:T(8,128)(2,1)}, bf16[256,128,4,32]{1,3,2,0:T(8,128)(2,1)}, u32[]{:S(2)}, u32[]{:S(2)}) %collective-permute-start.1) | collective-permute-done | bytes 8388640 | tf_op jit(solution)/shard_map/while/body/eval_jaxpr/ppermute | solution.py:89
  1835.3 94.1 %while.75 = (s32[]{:T(128)}, f32[8,32,4,128]{3,2,1,0:T(4,128)S(1)}, f32[8,32,4,128]{3,2,1,0:T(4,128)S(1)}, f32[8,32,4,128,32]{3,4,2,1,0:T(8,128)}, bf16[8,32,128...) while((s32[]{:T(128)}, f32[8,32,4,128]{3,2,1,0:T(4,128)S(1)}, ...), condition=%wide.region_10.10_spmd.clone, body=%wide.region_7.9_spmd.clone.sunk | while | flops 286326784 | bytes 38471784 | solution.py:43
  1960.5 82.5 %collective-permute-done = bf16[256,128,4,32]{1,3,2,0:T(8,128)(2,1)} collective-permute-done((bf16[256,128,4,32]{1,3,2,0:T(8,128)(2,1)}, bf16[256,128,4,32]{1,3,2,0:T(8,128)(2,1)}, u32[]{:S(2)}, u32[]{:S(2)}) %collective-permute-start) | collective-permute-done | bytes 8388640 | tf_op jit(solution)/shard_map/while/body/eval_jaxpr/ppermute | solution.py:88
  2043.0 89.9 %collective-permute-done.1 = bf16[256,128,4,32]{1,3,2,0:T(8,128)(2,1)} collective-permute-done((bf16[256,128,4,32]{1,3,2,0:T(8,128)(2,1)}, bf16[256,128,4,32]{1,3,2,0:T(8,128)(2,1)}, u32[]{:S(2)}, u32[]{:S(2)}) %collective-permute-start.1) | collective-permute-done | bytes 8388640 | tf_op jit(solution)/shard_map/while/body/eval_jaxpr/ppermute | solution.py:89
  2132.9 94.1 %while.75 = (s32[]{:T(128)}, f32[8,32,4,128]{3,2,1,0:T(4,128)S(1)}, f32[8,32,4,128]{3,2,1,0:T(4,128)S(1)}, f32[8,32,4,128,32]{3,4,2,1,0:T(8,128)}, bf16[8,32,128...) while((s32[]{:T(128)}, f32[8,32,4,128]{3,2,1,0:T(4,128)S(1)}, ...), condition=%wide.region_10.10_spmd.clone, body=%wide.region_7.9_spmd.clone.sunk | while | flops 286326784 | bytes 38471784 | solution.py:43
  2256.4 17.1 fusion.48
  (480 shorter events, 1023.9 us)
Async XLA Ops:
  6.5 2266.9 %copy-start = (bf16[128,128]{1,0:T(8,128)(2,1)S(1)}, bf16[128,128]{1,0:T(8,128)(2,1)}, u32[]{:S(2)}) copy-start(bf16[128,128]{1,0:T(8,128)(2,1)} %param.25) | copy-start | bytes 98308
  6.6 16.8 copy-start.13
  6.6 16.9 copy-start.12
  6.6 57.6 %all-gather.2.cloned.1.call-start = ((), (), s32[]{:S(2)}) async-start(), calls=%async_computation.1 | async-start | bytes 1310720 | tf_op jit(solution)/shard_map/all_gather | solution.py:63
  12.5 58.6 %copy-start.2 = (f32[256,128]{1,0:T(8,128)}, f32[256,128]{1,0:T(8,128)S(1)}, u32[]{:S(2)}) copy-start(f32[256,128]{1,0:T(8,128)S(1)} %broadcast_multiply_fusion) | copy-start | bytes 393220
  23.4 47.6 %copy-start.4 = (f32[256,128]{1,0:T(8,128)}, f32[256,128]{1,0:T(8,128)S(1)}, u32[]{:S(2)}) copy-start(f32[256,128]{1,0:T(8,128)S(1)} %add_rsqrt_fusion) | copy-start | bytes 393220
  50.1 20.1 copy-start.8
  50.1 20.2 copy-start.6
  50.1 21.0 copy-start.11
  64.2 21.0 all-to-all-start
  164.4 92.9 %collective-permute-start = (bf16[256,128,4,32]{1,3,2,0:T(8,128)(2,1)}, bf16[256,128,4,32]{1,3,2,0:T(8,128)(2,1)}, u32[]{:S(2)}, u32[]{:S(2)}) collective-permute-start(bf16[256,128,4,32]{1,3,2,0:T(8,128)(2,1)} %get-tuple-element.728), channel_id=1, source_target_pairs={{0,7},{1,0},{2,1},{3,2},{4,3},{5,4},{6,5},{7,6},{8,15},{9,8},{10,9... | collective-permute-start | bytes 25165832 | tf_op jit(solution)/shard_map/while/body/eval_jaxpr/ppermute | solution.py:88
  165.5 181.8 %collective-permute-start.1 = (bf16[256,128,4,32]{1,3,2,0:T(8,128)(2,1)}, bf16[256,128,4,32]{1,3,2,0:T(8,128)(2,1)}, u32[]{:S(2)}, u32[]{:S(2)}) collective-permute-start(bf16[256,128,4,32]{1,3,2,0:T(8,128)(2,1)} %get-tuple-element.729), channel_id=1, source_target_pairs={{0,7},{1,0},{2,1},{3,2},{4,3},{5,4},{6,5},{7,6},{8,15},{9,8},{10,9... | collective-permute-start | bytes 25165832 | tf_op jit(solution)/shard_map/while/body/eval_jaxpr/ppermute | solution.py:89
  462.1 92.9 %collective-permute-start = (bf16[256,128,4,32]{1,3,2,0:T(8,128)(2,1)}, bf16[256,128,4,32]{1,3,2,0:T(8,128)(2,1)}, u32[]{:S(2)}, u32[]{:S(2)}) collective-permute-start(bf16[256,128,4,32]{1,3,2,0:T(8,128)(2,1)} %get-tuple-element.728), channel_id=1, source_target_pairs={{0,7},{1,0},{2,1},{3,2},{4,3},{5,4},{6,5},{7,6},{8,15},{9,8},{10,9... | collective-permute-start | bytes 25165832 | tf_op jit(solution)/shard_map/while/body/eval_jaxpr/ppermute | solution.py:88
  463.1 181.7 %collective-permute-start.1 = (bf16[256,128,4,32]{1,3,2,0:T(8,128)(2,1)}, bf16[256,128,4,32]{1,3,2,0:T(8,128)(2,1)}, u32[]{:S(2)}, u32[]{:S(2)}) collective-permute-start(bf16[256,128,4,32]{1,3,2,0:T(8,128)(2,1)} %get-tuple-element.729), channel_id=1, source_target_pairs={{0,7},{1,0},{2,1},{3,2},{4,3},{5,4},{6,5},{7,6},{8,15},{9,8},{10,9... | collective-permute-start | bytes 25165832 | tf_op jit(solution)/shard_map/while/body/eval_jaxpr/ppermute | solution.py:89
  759.7 92.9 %collective-permute-start = (bf16[256,128,4,32]{1,3,2,0:T(8,128)(2,1)}, bf16[256,128,4,32]{1,3,2,0:T(8,128)(2,1)}, u32[]{:S(2)}, u32[]{:S(2)}) collective-permute-start(bf16[256,128,4,32]{1,3,2,0:T(8,128)(2,1)} %get-tuple-element.728), channel_id=1, source_target_pairs={{0,7},{1,0},{2,1},{3,2},{4,3},{5,4},{6,5},{7,6},{8,15},{9,8},{10,9... | collective-permute-start | bytes 25165832 | tf_op jit(solution)/shard_map/while/body/eval_jaxpr/ppermute | solution.py:88
  762.0 180.5 %collective-permute-start.1 = (bf16[256,128,4,32]{1,3,2,0:T(8,128)(2,1)}, bf16[256,128,4,32]{1,3,2,0:T(8,128)(2,1)}, u32[]{:S(2)}, u32[]{:S(2)}) collective-permute-start(bf16[256,128,4,32]{1,3,2,0:T(8,128)(2,1)} %get-tuple-element.729), channel_id=1, source_target_pairs={{0,7},{1,0},{2,1},{3,2},{4,3},{5,4},{6,5},{7,6},{8,15},{9,8},{10,9... | collective-permute-start | bytes 25165832 | tf_op jit(solution)/shard_map/while/body/eval_jaxpr/ppermute | solution.py:89
  1057.3 92.9 %collective-permute-start = (bf16[256,128,4,32]{1,3,2,0:T(8,128)(2,1)}, bf16[256,128,4,32]{1,3,2,0:T(8,128)(2,1)}, u32[]{:S(2)}, u32[]{:S(2)}) collective-permute-start(bf16[256,128,4,32]{1,3,2,0:T(8,128)(2,1)} %get-tuple-element.728), channel_id=1, source_target_pairs={{0,7},{1,0},{2,1},{3,2},{4,3},{5,4},{6,5},{7,6},{8,15},{9,8},{10,9... | collective-permute-start | bytes 25165832 | tf_op jit(solution)/shard_map/while/body/eval_jaxpr/ppermute | solution.py:88
  1060.8 179.3 %collective-permute-start.1 = (bf16[256,128,4,32]{1,3,2,0:T(8,128)(2,1)}, bf16[256,128,4,32]{1,3,2,0:T(8,128)(2,1)}, u32[]{:S(2)}, u32[]{:S(2)}) collective-permute-start(bf16[256,128,4,32]{1,3,2,0:T(8,128)(2,1)} %get-tuple-element.729), channel_id=1, source_target_pairs={{0,7},{1,0},{2,1},{3,2},{4,3},{5,4},{6,5},{7,6},{8,15},{9,8},{10,9... | collective-permute-start | bytes 25165832 | tf_op jit(solution)/shard_map/while/body/eval_jaxpr/ppermute | solution.py:89
  1354.9 92.9 %collective-permute-start = (bf16[256,128,4,32]{1,3,2,0:T(8,128)(2,1)}, bf16[256,128,4,32]{1,3,2,0:T(8,128)(2,1)}, u32[]{:S(2)}, u32[]{:S(2)}) collective-permute-start(bf16[256,128,4,32]{1,3,2,0:T(8,128)(2,1)} %get-tuple-element.728), channel_id=1, source_target_pairs={{0,7},{1,0},{2,1},{3,2},{4,3},{5,4},{6,5},{7,6},{8,15},{9,8},{10,9... | collective-permute-start | bytes 25165832 | tf_op jit(solution)/shard_map/while/body/eval_jaxpr/ppermute | solution.py:88
  1359.6 178.1 %collective-permute-start.1 = (bf16[256,128,4,32]{1,3,2,0:T(8,128)(2,1)}, bf16[256,128,4,32]{1,3,2,0:T(8,128)(2,1)}, u32[]{:S(2)}, u32[]{:S(2)}) collective-permute-start(bf16[256,128,4,32]{1,3,2,0:T(8,128)(2,1)} %get-tuple-element.729), channel_id=1, source_target_pairs={{0,7},{1,0},{2,1},{3,2},{4,3},{5,4},{6,5},{7,6},{8,15},{9,8},{10,9... | collective-permute-start | bytes 25165832 | tf_op jit(solution)/shard_map/while/body/eval_jaxpr/ppermute | solution.py:89
  1652.5 92.9 %collective-permute-start = (bf16[256,128,4,32]{1,3,2,0:T(8,128)(2,1)}, bf16[256,128,4,32]{1,3,2,0:T(8,128)(2,1)}, u32[]{:S(2)}, u32[]{:S(2)}) collective-permute-start(bf16[256,128,4,32]{1,3,2,0:T(8,128)(2,1)} %get-tuple-element.728), channel_id=1, source_target_pairs={{0,7},{1,0},{2,1},{3,2},{4,3},{5,4},{6,5},{7,6},{8,15},{9,8},{10,9... | collective-permute-start | bytes 25165832 | tf_op jit(solution)/shard_map/while/body/eval_jaxpr/ppermute | solution.py:88
  1658.4 176.9 %collective-permute-start.1 = (bf16[256,128,4,32]{1,3,2,0:T(8,128)(2,1)}, bf16[256,128,4,32]{1,3,2,0:T(8,128)(2,1)}, u32[]{:S(2)}, u32[]{:S(2)}) collective-permute-start(bf16[256,128,4,32]{1,3,2,0:T(8,128)(2,1)} %get-tuple-element.729), channel_id=1, source_target_pairs={{0,7},{1,0},{2,1},{3,2},{4,3},{5,4},{6,5},{7,6},{8,15},{9,8},{10,9... | collective-permute-start | bytes 25165832 | tf_op jit(solution)/shard_map/while/body/eval_jaxpr/ppermute | solution.py:89
  1950.2 92.9 %collective-permute-start = (bf16[256,128,4,32]{1,3,2,0:T(8,128)(2,1)}, bf16[256,128,4,32]{1,3,2,0:T(8,128)(2,1)}, u32[]{:S(2)}, u32[]{:S(2)}) collective-permute-start(bf16[256,128,4,32]{1,3,2,0:T(8,128)(2,1)} %get-tuple-element.728), channel_id=1, source_target_pairs={{0,7},{1,0},{2,1},{3,2},{4,3},{5,4},{6,5},{7,6},{8,15},{9,8},{10,9... | collective-permute-start | bytes 25165832 | tf_op jit(solution)/shard_map/while/body/eval_jaxpr/ppermute | solution.py:88
  1957.2 175.7 %collective-permute-start.1 = (bf16[256,128,4,32]{1,3,2,0:T(8,128)(2,1)}, bf16[256,128,4,32]{1,3,2,0:T(8,128)(2,1)}, u32[]{:S(2)}, u32[]{:S(2)}) collective-permute-start(bf16[256,128,4,32]{1,3,2,0:T(8,128)(2,1)} %get-tuple-element.729), channel_id=1, source_target_pairs={{0,7},{1,0},{2,1},{3,2},{4,3},{5,4},{6,5},{7,6},{8,15},{9,8},{10,9... | collective-permute-start | bytes 25165832 | tf_op jit(solution)/shard_map/while/body/eval_jaxpr/ppermute | solution.py:89
  (11 other events, 122.7 us)
Sparse Core Ops, SparseCore 0:
  36.0 23.1 all-gather.1
where the time goes:
time: 2300 us; the launch traced here: 2290 us
  waiting for transfers between devices  1230 us (53%)
  matrix products  551 us (24%)
  local copies, waits for them, and re-layouts  249 us (11%)
  other arithmetic  188 us (8%)
  starting transfers between devices  52.2 us (2%)
    ppermute x7, waiting for transfers between devices, col_step(): v_blk = lax.ppermute(v_blk, 'col', shift_pairs)  629 us
    ppermute x7, waiting for transfers between devices, col_step(): k_blk = lax.ppermute(k_blk, 'col', shift_pairs)  603 us
    dot_general x64, matrix products, one_group(): jnp.einsum('ihjk,ikhd->ihjd', att_weight.astype(jnp.bfloat16), v_rows, pr...  276 us
    dot_general x64, matrix products, one_group(): jnp.einsum('ijhd,ikhd->ihjk', q_rows, k_rows, preferred_element_type=jnp....  195 us
    reduce_sum x64, other arithmetic, one_group(): sum_new = sum_old * correction + jnp.sum(att_weight, axis=-1)  156 us
    while x14, local copies, waits for them, and re-layouts  145 us
    dynamic_slice x56, local copies, waits for them, and re-layouts, fold_keys(): lax.map(one_group, (q_groups, k_groups, v_groups, max_all, sum_all, acc_a...  102 us
  transfers between devices with their start and end apart: 16, of which 14 were waited for; matrix products, arithmetic and copies ran while one was open for 2% of the time, Pallas kernels for 0%

commit v1 on v0

v1 whole, which is shorter than its diff:
```python
import functools

import jax
import jax.numpy as jnp
from jax import lax
from jax.experimental import pallas as pl
from jax.experimental.pallas import tpu as pltpu
from jax.sharding import PartitionSpec as P

LN_EPS = 1e-5
MASK_NEG = -1e9
J_BLOCK = 256
VMEM_LIMIT = 60 * 1024 * 1024


def normalize(z_rows, ln_gamma, ln_beta):
    z_float = z_rows.astype(jnp.float32)
    row_mean = jnp.mean(z_float, axis=-1, keepdims=True)
    centered = z_float - row_mean
    row_var = jnp.mean(centered * centered, axis=-1, keepdims=True)
    return (centered * lax.rsqrt(row_var + LN_EPS) * ln_gamma + ln_beta).astype(jnp.bfloat16)


def dot_nt(lhs, rhs):
    return lax.dot_general(lhs, rhs, (((1,), (1,)), ((), ())), preferred_element_type=jnp.float32)


def bias_kernel(z_ref, gamma_ref, beta_ref, w_b_ref, out_ref, acc_ref):
    n_heads = out_ref.shape[0]
    rows_step, n_cols, pair_dim = z_ref.shape
    step = pl.program_id(0)
    normed = normalize(z_ref[...].reshape(rows_step * n_cols, pair_dim), gamma_ref[...], beta_ref[...])
    bias = dot_nt(w_b_ref[...], normed)
    for row in range(rows_step):
        for head in range(n_heads):
            acc_ref[head, pl.ds(step * rows_step + row, 1), :] = bias[head : head + 1, row * n_cols : (row + 1) * n_cols]

    @pl.when(step == pl.num_programs(0) - 1)
    def _():
        for head in range(n_heads):
            out_ref[head] = acc_ref[head].T.astype(jnp.bfloat16)


def attend_kernel(z_ref, mask_ref, bias_ref, gamma_ref, beta_ref, w_k_ref, w_qvg_ref, w_o_ref, out_ref, bias_f32, q_scr):
    n_src, _, n_cols, pair_dim = z_ref.shape
    n_heads, n_keys, n_query = bias_ref.shape
    head_dim = pair_dim // n_heads

    @pl.when(pl.program_id(0) == 0)
    def _():
        q_scr[...] = jnp.zeros_like(q_scr)
        for head in range(n_heads):
            for blk in range(0, n_keys, 128):
                key_add = jnp.where(mask_ref[blk : blk + 128, :] > 0, 0.0, MASK_NEG)
                bias_f32[head, blk : blk + 128, :] = bias_ref[head, blk : blk + 128, :].astype(jnp.float32) + key_add

    z_rows = z_ref[...].reshape(n_src * n_cols, pair_dim)
    normed = normalize(z_rows, gamma_ref[...], beta_ref[...])
    k_rows = jnp.dot(normed, w_k_ref[...], preferred_element_type=jnp.float32).astype(jnp.bfloat16)
    qvg = dot_nt(w_qvg_ref[...], normed)
    q_all = (qvg[:pair_dim] * head_dim ** -0.5).astype(jnp.bfloat16)
    v_all = qvg[pair_dim : 2 * pair_dim].astype(jnp.bfloat16)
    gate = jax.nn.sigmoid(qvg[2 * pair_dim :])
    for head in range(n_heads):
        q_scr[head, head * head_dim : (head + 1) * head_dim, :] = q_all[head * head_dim : (head + 1) * head_dim]
    for jb in range(0, n_query, J_BLOCK):
        gated = []
        for head in range(n_heads):
            rows = slice(head * head_dim, (head + 1) * head_dim)
            logits = jnp.dot(k_rows, q_scr[head, :, jb : jb + J_BLOCK], preferred_element_type=jnp.float32)
            logits = logits + bias_f32[head, :, jb : jb + J_BLOCK]
            top = jnp.max(logits, axis=0, keepdims=True)
            weights = jnp.exp(logits - top)
            total = jnp.sum(weights, axis=0, keepdims=True)
            attended = jnp.dot(v_all[rows], weights.astype(jnp.bfloat16), preferred_element_type=jnp.float32)
            gated.append((gate[rows, jb : jb + J_BLOCK] * (attended / total)).astype(jnp.bfloat16))
        u_cols = jnp.concatenate(gated, axis=0)
        update = lax.dot_general(u_cols, w_o_ref[...], (((0,), (0,)), ((), ())), preferred_element_type=jnp.float32)
        result = (z_rows[jb : jb + J_BLOCK].astype(jnp.float32) + update).astype(jnp.bfloat16)
        out_ref[jb // n_cols : (jb + J_BLOCK) // n_cols] = result.reshape(J_BLOCK // n_cols, 1, n_cols, pair_dim)


def solution(mesh):
    n_col_dev = mesh.shape["col"]
    tile_spec = P(("dp", "row"), "col", None)
    replicated = P()
    whole = pl.BlockSpec(memory_space=pltpu.VMEM)

    def local_fn(z_tile, res_mask, ln_gamma, ln_beta, w_q, w_k, w_v, w_g, w_b, w_o):
        n_rows_loc, n_cols, pair_dim = z_tile.shape
        n_heads = w_b.shape[1]
        rows_own = n_rows_loc // n_col_dev
        n_query = res_mask.shape[0]
        gamma, beta = ln_gamma[None, :], ln_beta[None, :]
        w_b_t = jnp.pad(w_b.T, ((0, 8 - n_heads), (0, 0)))
        rows_step = 16
        bias_t = pl.pallas_call(
            bias_kernel,
            grid=(n_rows_loc // rows_step,),
            in_specs=[pl.BlockSpec((rows_step, n_cols, pair_dim), lambda i: (i, 0, 0)), whole, whole, whole],
            out_specs=pl.BlockSpec((n_heads, n_cols, n_rows_loc), lambda i: (0, 0, 0)),
            out_shape=jax.ShapeDtypeStruct((n_heads, n_cols, n_rows_loc), jnp.bfloat16),
            scratch_shapes=[pltpu.VMEM((n_heads, n_rows_loc, n_cols), jnp.float32)],
            compiler_params=pltpu.CompilerParams(vmem_limit_bytes=VMEM_LIMIT),
        )(z_tile, gamma, beta, w_b_t)
        bias_t = lax.all_gather(bias_t, "col", axis=1, tiled=True)
        bias_t = lax.all_gather(bias_t, "row", axis=2, tiled=True)
        z_own = lax.all_to_all(z_tile.reshape(n_col_dev, rows_own, n_cols, pair_dim), "col", 0, 0, tiled=True)
        w_qvg_t = jnp.concatenate([w_q, w_v, w_g], axis=1).T
        blk = pl.BlockSpec((n_col_dev, 1, n_cols, pair_dim), lambda i: (0, i, 0, 0))
        out = pl.pallas_call(
            attend_kernel,
            grid=(rows_own,),
            in_specs=[blk, whole, whole, whole, whole, whole, whole, whole],
            out_specs=blk,
            out_shape=jax.ShapeDtypeStruct(z_own.shape, jnp.bfloat16),
            scratch_shapes=[
                pltpu.VMEM((n_heads, n_query, n_query), jnp.float32),
                pltpu.VMEM((n_heads, pair_dim, n_query), jnp.bfloat16),
            ],
            compiler_params=pltpu.CompilerParams(vmem_limit_bytes=VMEM_LIMIT),
        )(z_own, res_mask[:, None], bias_t, gamma, beta, w_k, w_qvg_t, w_o)
        out = lax.all_to_all(out, "col", 0, 0, tiled=True)
        return out.reshape(n_rows_loc, n_cols, pair_dim)

    return jax.shard_map(
        local_fn,
        mesh=mesh,
        in_specs=(tile_spec, P("dp"), replicated, replicated, replicated, replicated, replicated, replicated, replicated, replicated),
        out_specs=tile_spec,
        check_vma=False,
    )
```

time: 2300 us -> 666 us (0.29)
  waiting for transfers between devices: 1230 us -> 119 us
  matrix products: 551 us -> 0 us
  Pallas kernels: 0 us -> 414 us
  local copies, waits for them, and re-layouts: 249 us -> 13.2 us
  other arithmetic: 188 us -> 0.66 us
  blocking collectives: 0 us -> 100 us
  starting transfers between devices: 52.2 us -> 5.32 us
    ppermute x14 -> x0, waiting for transfers between devices: 1230 us -> none  [the longest x7 629 us: col_step(): v_blk = lax.ppermute(v_blk, 'col', shift_pairs)]
    dot_general x134 -> x0, matrix products: 551 us -> none  [the longest x64 276 us: one_group(): jnp.einsum('ihjk,ikhd->ihjd', att_weight.astype(jnp.bfloat16), v_rows, pr...]
    pallas_call x0 -> x2, Pallas kernels: none -> 414 us  [the longest x1 398 us: local_fn(): pl.pallas_call(attend_kernel, grid=(rows_own,), in_specs=[blk, whole, who...]
    reduce_sum x66 -> x0, other arithmetic: 173 us -> none  [the longest x64 156 us: one_group(): sum_new = sum_old * correction + jnp.sum(att_weight, axis=-1)]
    while x14 -> x0, local copies, waits for them, and re-layouts: 145 us -> none
    dynamic_slice x64 -> x0, local copies, waits for them, and re-layouts: 103 us -> none  [the longest x56 102 us: fold_keys(): lax.map(one_group, (q_groups, k_groups, v_groups, max_all, sum_all, acc_a...]
    all_to_all x0 -> x1, blocking collectives: none -> 100 us  [local_fn(): out = lax.all_to_all(out, 'col', 0, 0, tiled=True)]
    all_to_all x1, waiting for transfers between devices: 0.01 us -> 91.5 us  [local_fn(): lax.all_to_all(z_tile.reshape(n_col_dev, rows_own, n_cols, pair_dim), 'co...]
  transfers between devices with their start and end apart: 16 -> 3, of which waited for: 14 -> 2; matrix products, arithmetic and copies ran while one was open for 2% -> 0% of each run, Pallas kernels for 0% -> 0%
where the time goes in v1:
time: 666 us
  Pallas kernels  414 us (62%)
  waiting for transfers between devices  119 us (18%)
  blocking collectives  100 us (15%)
  between operations  13.5 us (2%)
  local copies, waits for them, and re-layouts  13.2 us (2%)
    pallas_call x1, Pallas kernels, local_fn(): pl.pallas_call(attend_kernel, grid=(rows_own,), in_specs=[blk, whole, who...  398 us
    all_to_all x1, blocking collectives, local_fn(): out = lax.all_to_all(out, 'col', 0, 0, tiled=True)  100 us
    all_to_all x1, waiting for transfers between devices, local_fn(): lax.all_to_all(z_tile.reshape(n_col_dev, rows_own, n_cols, pair_dim), 'co...  91.5 us
    all_gather x1, waiting for transfers between devices, local_fn(): bias_t = lax.all_gather(bias_t, 'col', axis=1, tiled=True)  26.9 us
    pallas_call x1, Pallas kernels, local_fn(): pl.pallas_call(bias_kernel, grid=(n_rows_loc // rows_step,), in_specs=[pl...  16.3 us
  transfers between devices with their start and end apart: 3, of which 2 were waited for; matrix products, arithmetic and copies ran while one was open for 0% of the time, Pallas kernels for 0%

profile of v1, /device:TPU:97, one launch (start us, length us, event | category | flops | bytes accessed | tf_op | source)
XLA Modules:
  0.0 665.5 jit_solution(11099656176078426918)
XLA Ops:
  6.5 0.0 all-gather.3.cloned.1.call-start
  6.6 1.3 pad.4.w_b_ref
  7.8 16.3 %shard_map.100 = bf16[4,128,256]{2,1,0:T(8,128)(2,1)} custom-call(bf16[256,128,128]{2,1,0:T(8,128)(2,1)} %z_ref.1, f32[1,128]{1,0:T(1,128)} %bitcast.11, f32[1,128]{1,0:T(1,128)} %bitcast.13, bf16[8,128]{1,0:T(8,128)(2,1)} %pad.4.w_b_ref), custom_call_target="tpu_custom_call" | custom-call | tf_op jit(solution)/shard_map/pallas_call | solution.py:97
  24.2 0.1 all-gather.3.cloned.1.call-update
  24.2 0.1 all-gather.5.cloned.1.call-start
  24.3 26.9 %all-gather.3.cloned.1.call-done = bf16[4,1024,256]{2,1,0:T(8,128)(2,1)} async-done(((bf16[4,128,256]{2,1,0:T(8,128)(2,1)}), bf16[4,1024,256]{2,1,0:T(8,128)(2,1)}) %all-gather.3.cloned.1.call-update) | async-done | bytes 2097168 | tf_op jit(solution)/shard_map/all_gather | solution.py:106
  51.2 0.1 all-gather.5.cloned.1.call-update
  51.2 0.0 copy-start
  51.3 0.0 copy-start.1
  51.3 0.0 copy-start.2
  51.3 0.0 copy-start.3
  51.3 5.3 all-to-all-start
  56.6 0.0 copy-done
  56.6 0.1 copy.14
  56.7 0.0 copy-done.1
  56.7 0.1 copy.15
  56.8 0.0 copy-done.2
  56.8 0.1 copy.16
  56.9 1.0 copy.17.mask_ref
  58.0 0.7 maximum_bitcast_fusion.w_qvg_ref
  58.6 91.5 %all-to-all-done.z_ref = bf16[8,32,128,128]{3,2,1,0:T(8,128)(2,1)} async-done(((bf16[8,32,128,128]{3,2,1,0:T(8,128)(2,1)}), bf16[8,32,128,128]{3,2,1,0:T(8,128)(2,1)}, u32[]{:S(2)}, u32[]{:S(2)}) %all-to-all-start) | async-done | bytes 8388640 | tf_op jit(solution)/shard_map/all_to_all | solution.py:108
  150.2 397.9 %shard_map.101 = bf16[8,32,128,128]{3,2,1,0:T(8,128)(2,1)} custom-call(bf16[8,32,128,128]{3,2,1,0:T(8,128)(2,1)} %all-to-all-done.z_ref, s32[1024,1]{1,0:T(8,128)} %copy.17.mask_ref, bf16[4,1024,1024]{2,1,0:T(8,128)(2,1)} %all-gather.5.cloned.1.call-done.bias_ref, f32[1,128]{1,0:T(1,128)} %bitcast.12, f32[1,128]{1,0:T(1,128)} %bitcast.14, ...), custom_call_target="tpu_custom_call" | custom-call | tf_op jit(solution)/shard_map/pallas_call | solution.py:111
  548.0 100.1 %all_to_all.10 = bf16[8,32,128,128]{3,2,1,0:T(8,128)(2,1)} all-to-all(bf16[8,32,128,128]{3,2,1,0:T(8,128)(2,1)} %shard_map.101), channel_id=1, replica_groups=mesh['dp'=1,'row'=4,'col'=8] {'col'}, dimensions={0} | all-to-all | bytes 16777216 | tf_op jit(solution)/shard_map/all_to_all | solution.py:123
  648.2 10.5 %copy.19 = bf16[256,128,128]{2,1,0:T(8,128)(2,1)} copy(bf16[256,128,128]{2,1,0:T(8,128)(2,1)} %bitcast.9) | data formatting | bytes 16777216
  (2 shorter events, 0.0 us)
Async XLA Ops:
  6.5 44.6 %all-gather.3.cloned.1.call-start = ((), (), s32[]{:S(2)}) async-start(), calls=%async_computation.2 | async-start | bytes 2359296 | tf_op jit(solution)/shard_map/all_gather | solution.py:106
  24.2 125.9 %all-gather.5.cloned.1.call-start = ((), (), s32[]{:S(2)}) async-start(), calls=%async_computation.3 | async-start | bytes 10485760 | tf_op jit(solution)/shard_map/all_gather | solution.py:107
  51.2 5.3 copy-start
  51.3 5.4 copy-start.1
  51.3 5.5 copy-start.2
  51.3 5.6 copy-start.3
  51.3 98.9 %all-to-all-start = ((bf16[8,32,128,128]{3,2,1,0:T(8,128)(2,1)}), bf16[8,32,128,128]{3,2,1,0:T(8,128)(2,1)}, u32[]{:S(2)}, u32[]{:S(2)}) async-start(bf16[8,32,128,128]{3,2,1,0:T(8,128)(2,1)} %bitcast.8), calls=%async_computation | async-start | bytes 16777216 | tf_op jit(solution)/shard_map/all_to_all | solution.py:108
Sparse Core Ops, SparseCore 0:
  24.3 26.8 all-gather.2
  52.7 83.0 all-gather.4

commit v2 on v1

--- a/solution.py
+++ b/solution.py
@@ -41,7 +41,7 @@
             out_ref[head] = acc_ref[head].T.astype(jnp.bfloat16)
 
 
-def attend_kernel(z_ref, mask_ref, bias_ref, gamma_ref, beta_ref, w_k_ref, w_qvg_ref, w_o_ref, out_ref, bias_f32, q_scr):
+def attend_kernel(z_ref, mask_ref, bias_ref, gamma_ref, beta_ref, w_k_ref, w_qvg_ref, w_o_ref, out_ref, bias_f32, q_scr, gate_scr):
     n_src, _, n_cols, pair_dim = z_ref.shape
     n_heads, n_keys, n_query = bias_ref.shape
     head_dim = pair_dim // n_heads
@@ -60,24 +60,319 @@
     qvg = dot_nt(w_qvg_ref[...], normed)
     q_all = (qvg[:pair_dim] * head_dim ** -0.5).astype(jnp.bfloat16)
     v_all = qvg[pair_dim : 2 * pair_dim].astype(jnp.bfloat16)
-    gate = jax.nn.sigmoid(qvg[2 * pair_dim :])
     for head in range(n_heads):
         q_scr[head, head * head_dim : (head + 1) * head_dim, :] = q_all[head * head_dim : (head + 1) * head_dim]
-    for jb in range(0, n_query, J_BLOCK):
+    gate_scr[...] = jax.nn.sigmoid(qvg[2 * pair_dim :])
+
+    def one_block(blk_idx, _):
+        jb = pl.multiple_of(blk_idx * J_BLOCK, J_BLOCK)
         gated = []
         for head in range(n_heads):
             rows = slice(head * head_dim, (head + 1) * head_dim)
-            logits = jnp.dot(k_rows, q_scr[head, :, jb : jb + J_BLOCK], preferred_element_type=jnp.float32)
-            logits = logits + bias_f32[head, :, jb : jb + J_BLOCK]
+            logits = jnp.dot(k_rows, q_scr[head, :, pl.ds(jb, J_BLOCK)], preferred_element_type=jnp.float32)
+            logits = logits + bias_f32[head, :, pl.ds(jb, J_BLOCK)]
             top = jnp.max(logits, axis=0, keepdims=True)
             weights = jnp.exp(logits - top)
             total = jnp.sum(weights, axis=0, keepdims=True)
             attended = jnp.dot(v_all[rows], weights.astype(jnp.bfloat16), preferred_element_type=jnp.float32)
-            gated.append((gate[rows, jb : jb + J_BLOCK] * (attended / total)).astype(jnp.bfloat16))
+            gated.append((gate_scr[rows, pl.ds(jb, J_BLOCK)] * (attended / total)).astype(jnp.bfloat16))
         u_cols = jnp.concatenate(gated, axis=0)
         update = lax.dot_general(u_cols, w_o_ref[...], (((0,), (0,)), ((), ())), preferred_element_type=jnp.float32)
-        result = (z_rows[jb : jb + J_BLOCK].astype(jnp.float32) + update).astype(jnp.bfloat16)
-        out_ref[jb // n_cols : (jb + J_BLOCK) // n_cols] = result.reshape(J_BLOCK // n_cols, 1, n_cols, pair_dim)
+        n_blk = J_BLOCK // n_cols
+        z_blk = z_ref[pl.ds(blk_idx * n_blk, n_blk)].reshape(J_BLOCK, pair_dim).astype(jnp.float32)
+        out_ref[pl.ds(blk_idx * n_blk, n_blk)] = (z_blk + update).astype(jnp.bfloat16).reshape(n_blk, 1, n_cols, pair_dim)
+        return 0
+
+    lax.fori_loop(0, n_query // J_BLOCK, one_block, 0)
+
+
+MESH = pl.DeviceIdType.MESH
+LOG2E = 1.4426950408889634
+STEP_ROWS = 4
+KEY_CHUNK = 416
+
+
+def fold8(values, op):
+    return op(values.reshape(values.shape[0] // 8, 8, values.shape[1]), axis=0)
+
+
+def fused_kernel(
+    n_dev, n_row_dev, n_heads, n_used,
+    z_hbm, mask_ref, gamma_ref, beta_ref, w_b_ref, w_k_ref, w_qvg_ref, w_o_ref, eye_ref,
+    out_hbm,
+    z_in, b_acc, b_all, z_rows, a_scr, k_scr, q_scr, v_scr, g_scr, s_scr, u_scr, o_scr,
+    in_sem, own_sem, z_send, z_recv, bx_send, bx_recv, by_send, by_recv, bd_send, bd_recv, o_send, o_recv, o_own,
+):
+    me, row = lax.axis_index("col"), lax.axis_index("row")
+    n_rows_loc, n_cols, pair_dim = z_hbm.shape
+    head_dim = pair_dim // n_heads
+    rows_own = n_rows_loc // n_dev
+    n_steps = rows_own // STEP_ROWS
+    n_chip = n_dev // 2
+    blk_rows = n_rows_loc // n_cols
+    chunk = z_in.shape[1]
+    n_chunks = n_rows_loc // chunk
+    col_at = lambda d: lax.rem(me + d + n_dev, n_dev)
+    row_at = lambda d: lax.rem(row + d + n_row_dev, n_row_dev)
+    partner = me + 1 - 2 * lax.rem(me, 2)
+
+    barrier = pltpu.get_barrier_semaphore()
+    for d in range(1, n_dev):
+        pl.semaphore_signal(barrier, inc=1, device_id={"col": col_at(d)}, device_id_type=MESH)
+    for d in range(1, n_row_dev):
+        pl.semaphore_signal(barrier, inc=1, device_id={"row": row_at(d)}, device_id_type=MESH)
+    pl.semaphore_wait(barrier, n_dev + n_row_dev - 2)
+
+    def z_copy(step, d, to, at):
+        return pltpu.make_async_remote_copy(
+            z_hbm.at[pl.ds(to * rows_own + step * STEP_ROWS, STEP_ROWS)], z_rows.at[at, pl.ds(step * STEP_ROWS, STEP_ROWS)],
+            z_send.at[step, d], z_recv.at[step, d], device_id={"col": to}, device_id_type=MESH)
+
+    def start_z(step):
+        for d in range(1, n_dev):
+            z_copy(step, d, col_at(d), me).start()
+
+    def b_tile(src_row, src_col):
+        return b_all.at[pl.ds(src_row * blk_rows, blk_rows), :, pl.ds(pl.multiple_of(src_col * n_cols, n_cols), n_cols), :]
+
+    def b_copy(src_row, src_col, send, recv, target):
+        tile = b_tile(src_row, src_col)
+        return pltpu.make_async_remote_copy(tile, tile, send, recv, device_id=target, device_id_type=MESH)
+
+    def bx(d, src_col):
+        return b_copy(row, src_col, bx_send.at[d], bx_recv.at[d], {"col": col_at(2 * d)})
+
+    def by(t, e, src_row):
+        return b_copy(src_row, col_at(-2 * t), by_send.at[t, e], by_recv.at[t, e], {"row": row_at(e)})
+
+    def bd(t, e, base):
+        return b_copy(row_at(-e), lax.rem(base - 2 * t + n_dev, n_dev), bd_send.at[t, e], bd_recv.at[t, e], {"col": partner})
+
+    def out_copy(step, d, to, at):
+        return pltpu.make_async_remote_copy(
+            o_scr.at[lax.rem(step, 2), to], out_hbm.at[pl.ds(at * rows_own + step * STEP_ROWS, STEP_ROWS)],
+            o_send.at[lax.rem(step, 2), d], o_recv.at[step, d], device_id={"col": to}, device_id_type=MESH)
+
+    def out_own(step):
+        return pltpu.make_async_copy(
+            o_scr.at[lax.rem(step, 2), me], out_hbm.at[pl.ds(me * rows_own + step * STEP_ROWS, STEP_ROWS)], o_own.at[lax.rem(step, 2)])
+
+    own_rows = pltpu.make_async_copy(z_hbm.at[pl.ds(me * rows_own, rows_own)], z_rows.at[me], own_sem)
+    own_rows.start()
+    start_z(0)
+    start_z(1)
+
+    def load_chunk(idx):
+        return pltpu.make_async_copy(z_hbm.at[pl.ds(idx * chunk, chunk)], z_in.at[lax.rem(idx, 2)], in_sem.at[lax.rem(idx, 2)])
+
+    load_chunk(0).start()
+
+    def bias_chunk(idx, _):
+        @pl.when(idx + 1 < n_chunks)
+        def _():
+            load_chunk(idx + 1).start()
+
+        load_chunk(idx).wait()
+        normed = normalize(z_in[lax.rem(idx, 2)].reshape(chunk * n_cols, pair_dim), gamma_ref[...], beta_ref[...])
+        bias = dot_nt(w_b_ref[...], normed)
+        for r in range(chunk):
+            for head in range(n_heads):
+                b_acc[head, pl.ds(idx * chunk + r, 1), :] = bias[head : head + 1, r * n_cols : (r + 1) * n_cols]
+        return 0
+
+    lax.fori_loop(0, n_chunks, bias_chunk, 0)
+    own_cols = pl.ds(pl.multiple_of(me * n_cols, n_cols), n_cols)
+    for blk in range(blk_rows):
+        for head in range(n_heads):
+            tile = b_acc[head, blk * n_cols : (blk + 1) * n_cols, :].T
+            b_all[row * blk_rows + blk, head, own_cols, :] = jnp.where(mask_ref[...] > 0, tile, MASK_NEG).astype(jnp.bfloat16)
+
+    def clear(idx, _):
+        q_scr[idx] = jnp.zeros(q_scr.shape[1:], q_scr.dtype)
+        return 0
+
+    lax.fori_loop(0, q_scr.shape[0], clear, 0)
+
+    for d in range(1, n_chip):
+        bx(d, me).start()
+    for e in range(1, n_row_dev):
+        by(0, e, row).start()
+    bd(0, 0, me).start()
+    for step in range(2, n_steps):
+        start_z(step)
+    for t in range(1, n_chip):
+        bx(t, col_at(-2 * t)).wait_recv()
+        for e in range(1, n_row_dev):
+            by(t, e, row).start()
+        bd(t, 0, me).start()
+
+    def prologue(step):
+        for d in range(1, n_dev):
+            z_copy(step, d, me, col_at(-d)).wait_recv()
+        for r in range(STEP_ROWS):
+            normed = normalize(z_rows[:, step * STEP_ROWS + r].reshape(n_dev * n_cols, pair_dim), gamma_ref[...], beta_ref[...])
+            a_scr[r] = normed
+            qvg = dot_nt(w_qvg_ref[...], normed)
+            pair, half = r // 2, r % 2
+            q_all = (qvg[:pair_dim] * head_dim ** -0.5).astype(jnp.bfloat16)
+            v_all = qvg[pair_dim : 2 * pair_dim].astype(jnp.bfloat16)
+            gate = jax.nn.sigmoid(qvg[2 * pair_dim :])
+            for head in range(n_heads):
+                hs = slice(head * head_dim, (head + 1) * head_dim)
+                v_scr[pair, head, half * head_dim : (half + 1) * head_dim, :] = v_all[hs]
+                for jb in range(n_dev):
+                    js = slice(jb * n_cols, (jb + 1) * n_cols)
+                    ls = slice(half * n_cols, (half + 1) * n_cols)
+                    q_scr[jb * 2 + pair, head, r * head_dim : (r + 1) * head_dim, ls] = q_all[hs, js]
+                    g_scr[jb * 2 + pair, head, :, ls] = gate[hs, js]
+        for k0 in range(0, n_used, 128):
+            kn = min(128, n_used - k0)
+            a_cat = jnp.concatenate([a_scr[r, k0 : k0 + kn, :] for r in range(STEP_ROWS)], axis=1)
+            k_all = jnp.dot(a_cat, w_k_ref[...], preferred_element_type=jnp.float32).astype(jnp.bfloat16)
+            for head in range(n_heads):
+                k_scr[head, k0 : k0 + kn, :] = k_all[:, head * pair_dim : (head + 1) * pair_dim]
+
+    key_blocks = [(k0, min(KEY_CHUNK, n_used - k0)) for k0 in range(0, n_used, KEY_CHUNK)]
+    n_units = n_dev * 2
+
+    def logits_of(head, unit, slot, k0, kn, top):
+        lhs = jnp.concatenate([k_scr[head, k0 : k0 + kn, :], b_all[lax.div(unit, 2), head, k0 : k0 + kn, :]], axis=1)
+        rhs = jnp.concatenate([q_scr[unit, head], eye_ref[...]], axis=0)
+        scaled = jnp.dot(lhs, rhs, preferred_element_type=jnp.float32) * LOG2E
+        s_scr[slot, k0 : k0 + kn, :] = scaled
+        new_top = fold8(scaled, jnp.max)
+        return new_top if top is None else jnp.maximum(top, new_top)
+
+    def update_unit(step, unit):
+        jb, pair = lax.div(unit, 2), lax.rem(unit, 2)
+        update = lax.dot_general(u_scr[pair], w_o_ref[...], (((0,), (0,)), ((), ())), preferred_element_type=jnp.float32)
+        for half in range(2):
+            r = pair * 2 + half
+            z_blk = z_rows[jb, step * STEP_ROWS + r].astype(jnp.float32)
+            o_scr[lax.rem(step, 2), jb, r] = (z_blk + update[half * n_cols : (half + 1) * n_cols]).astype(jnp.bfloat16)
+
+    def attend(step):
+        def one_unit(unit, top):
+            pair = lax.rem(unit, 2)
+            unit_next = jnp.minimum(unit + 1, n_units - 1)
+            for head in range(n_heads):
+                head_next, from_unit = (head + 1, unit) if head + 1 < n_heads else (0, unit_next)
+                top_row = jnp.max(top, axis=0, keepdims=True)
+                top_next = total = attended = None
+                for k0, kn in key_blocks:
+                    top_next = logits_of(head_next, from_unit, (head + 1) % 2, k0, kn, top_next)
+                    weights = jnp.exp2(s_scr[head % 2, k0 : k0 + kn, :] - top_row)
+                    part = fold8(weights, jnp.sum)
+                    total = part if total is None else total + part
+                    prod = jnp.dot(v_scr[pair, head, :, k0 : k0 + kn], weights.astype(jnp.bfloat16), preferred_element_type=jnp.float32)
+                    attended = prod if attended is None else attended + prod
+                inv = 1.0 / jnp.sum(total, axis=0, keepdims=True)
+                picked = jnp.concatenate([attended[:head_dim, :n_cols], attended[head_dim:, n_cols:]], axis=1)
+                u_scr[pair, head * head_dim : (head + 1) * head_dim, :] = (g_scr[unit, head] * (picked * inv)).astype(jnp.bfloat16)
+                top = top_next
+                if head == 0:
+                    update_unit(step, jnp.maximum(unit - 1, 0))
+            return top
+
+        top = None
+        for k0, kn in key_blocks:
+            top = logits_of(0, 0, 0, k0, kn, top)
+        lax.fori_loop(0, n_units, one_unit, top)
+        update_unit(step, n_units - 1)
+
+    own_rows.wait()
+    prologue(0)
+    for t in range(n_chip):
+        for e in range(1, n_row_dev):
+            by(t, e, row_at(-e)).wait_recv()
+            bd(t, e, me).start()
+    for t in range(n_chip):
+        for e in range(n_row_dev):
+            bd(t, e, partner).wait_recv()
+
+    def one_step(step, _):
+        @pl.when(step >= 2)
+        def _():
+            for d in range(1, n_dev):
+                out_copy(step - 2, d, col_at(d), me).wait_send()
+            out_own(step - 2).wait()
+
+        @pl.when(step >= 1)
+        def _():
+            prologue(step)
+
+        attend(step)
+        for d in range(1, n_dev):
+            out_copy(step, d, col_at(d), me).start()
+        out_own(step).start()
+        return 0
+
+    lax.fori_loop(0, n_steps, one_step, 0)
+
+    for step in range(n_steps - 2, n_steps):
+        for d in range(1, n_dev):
+            out_copy(step, d, col_at(d), me).wait_send()
+        out_own(step).wait()
+    for d in range(1, n_chip):
+        bx(d, me).wait_send()
+    for t in range(n_chip):
+        for e in range(1, n_row_dev):
+            by(t, e, row).wait_send()
+        for e in range(n_row_dev):
+            bd(t, e, me).wait_send()
+
+    def drain(step, _):
+        for d in range(1, n_dev):
+            z_copy(step, d, col_at(d), me).wait_send()
+            out_copy(step, d, me, col_at(-d)).wait_recv()
+        return 0
+
+    lax.fori_loop(0, n_steps, drain, 0)
+
+
+def fused_path(mesh, z_tile, res_mask, ln_gamma, ln_beta, w_q, w_k, w_v, w_g, w_b, w_o):
+    n_dev, n_row_dev = mesh.shape["col"], mesh.shape["row"]
+    n_rows_loc, n_cols, pair_dim = z_tile.shape
+    n_heads = w_b.shape[1]
+    n_query = res_mask.shape[0]
+    n_used = -(-(n_query - n_query // 5) // 64) * 64
+    rows_own = n_rows_loc // n_dev
+    n_steps = rows_own // STEP_ROWS
+    head_dim = pair_dim // n_heads
+    mask_own = lax.dynamic_slice_in_dim(res_mask, lax.axis_index("col") * n_cols, n_cols)[:, None]
+    w_b_t = jnp.pad(w_b.T, ((0, 8 - n_heads), (0, 0)))
+    w_qvg_t = jnp.concatenate([w_q, w_v, w_g], axis=1).T
+    spread = jnp.eye(STEP_ROWS, dtype=w_k.dtype)
+    w_k_wide = jnp.einsum("rs,chd->rchsd", spread, w_k.reshape(pair_dim, n_heads, head_dim)).reshape(STEP_ROWS * pair_dim, n_heads * pair_dim)
+    eye = jnp.tile(jnp.eye(n_cols, dtype=jnp.bfloat16), (1, 2))
+    whole = pl.BlockSpec(memory_space=pltpu.VMEM)
+    hbm = pl.BlockSpec(memory_space=pl.ANY)
+    bf16, f32, dma = jnp.bfloat16, jnp.float32, pltpu.SemaphoreType.DMA
+    n_units = n_dev * 2
+    return pl.pallas_call(
+        functools.partial(fused_kernel, n_dev, n_row_dev, n_heads, n_used),
+        in_specs=[hbm] + [whole] * 8,
+        out_specs=hbm,
+        out_shape=jax.ShapeDtypeStruct(z_tile.shape, bf16),
+        scratch_shapes=[
+            pltpu.VMEM((2, 16, n_cols, pair_dim), bf16),
+            pltpu.VMEM((n_heads, n_rows_loc, n_cols), f32),
+            pltpu.VMEM((n_query // n_cols, n_heads, n_query, n_cols), bf16),
+            pltpu.VMEM((n_dev, rows_own, n_cols, pair_dim), bf16),
+            pltpu.VMEM((STEP_ROWS, n_query, pair_dim), bf16),
+            pltpu.VMEM((n_heads, n_query, STEP_ROWS * head_dim), bf16),
+            pltpu.VMEM((n_units, n_heads, STEP_ROWS * head_dim, 2 * n_cols), bf16),
+            pltpu.VMEM((2, n_heads, 2 * head_dim, n_query), bf16),
+            pltpu.VMEM((n_units, n_heads, head_dim, 2 * n_cols), f32),
+            pltpu.VMEM((2, n_used, 2 * n_cols), f32),
+            pltpu.VMEM((2, pair_dim, 2 * n_cols), bf16),
+            pltpu.VMEM((2, n_dev, STEP_ROWS, n_cols, pair_dim), bf16),
+            dma((2,)), dma, dma((n_steps, n_dev)), dma((n_steps, n_dev)),
+            dma((n_dev // 2,)), dma((n_dev // 2,)), dma((n_dev // 2, n_row_dev)), dma((n_dev // 2, n_row_dev)),
+            dma((n_dev // 2, n_row_dev)), dma((n_dev // 2, n_row_dev)), dma((2, n_dev)), dma((n_steps, n_dev)), dma((2,)),
+        ],
+        compiler_params=pltpu.CompilerParams(collective_id=0, has_side_effects=True, vmem_limit_bytes=VMEM_LIMIT),
+    )(z_tile, mask_own, ln_gamma[None, :], ln_beta[None, :], w_b_t, w_k_wide, w_qvg_t, w_o, eye)
 
 
 def solution(mesh):
@@ -86,7 +381,7 @@
     replicated = P()
     whole = pl.BlockSpec(memory_space=pltpu.VMEM)
 
-    def local_fn(z_tile, res_mask, ln_gamma, ln_beta, w_q, w_k, w_v, w_g, w_b, w_o):
+    def whole_keys_path(z_tile, res_mask, ln_gamma, ln_beta, w_q, w_k, w_v, w_g, w_b, w_o):
         n_rows_loc, n_cols, pair_dim = z_tile.shape
         n_heads = w_b.shape[1]
         rows_own = n_rows_loc // n_col_dev
@@ -117,11 +412,20 @@
             scratch_shapes=[
                 pltpu.VMEM((n_heads, n_query, n_query), jnp.float32),
                 pltpu.VMEM((n_heads, pair_dim, n_query), jnp.bfloat16),
+                pltpu.VMEM((pair_dim, n_query), jnp.float32),
             ],
             compiler_params=pltpu.CompilerParams(vmem_limit_bytes=VMEM_LIMIT),
         )(z_own, res_mask[:, None], bias_t, gamma, beta, w_k, w_qvg_t, w_o)
         out = lax.all_to_all(out, "col", 0, 0, tiled=True)
         return out.reshape(n_rows_loc, n_cols, pair_dim)
+
+    def local_fn(*args):
+        _, _, ln_gamma, ln_beta, w_q, w_k, _, _, w_b, _ = args
+        pair_dim, n_heads = w_b.shape
+        largest = (pair_dim ** 0.5 * jnp.abs(ln_gamma) + jnp.abs(ln_beta))[:, None]
+        bound = lambda weight: jnp.sum(largest * jnp.abs(weight.astype(jnp.float32)), axis=0)
+        logit_bound = jnp.sum(bound(w_q) * bound(w_k)) + jnp.max(bound(w_b))
+        return lax.cond(logit_bound < 1e8, functools.partial(fused_path, mesh), whole_keys_path, *args)
 
     return jax.shard_map(
         local_fn,

time: 666 us -> 314 us (0.47)
  Pallas kernels: 414 us -> 275 us
  waiting for transfers between devices: 119 us -> 0 us
  blocking collectives: 100 us -> 0 us
    pallas_call x2 -> x1, Pallas kernels: 414 us -> 275 us  [fused_path(): pl.pallas_call(functools.partial(fused_kernel, n_dev, n_row_dev, n_heads,...]
    all_to_all x1 -> x0, blocking collectives: 100 us -> none  [local_fn(): out = lax.all_to_all(out, 'col', 0, 0, tiled=True)]
    all_to_all x1 -> x0, waiting for transfers between devices: 91.5 us -> none  [local_fn(): lax.all_to_all(z_tile.reshape(n_col_dev, rows_own, n_cols, pair_dim), 'co...]
    all_gather x2 -> x0, waiting for transfers between devices: 26.9 us -> none  [the longest x1 26.9 us: local_fn(): bias_t = lax.all_gather(bias_t, 'col', axis=1, tiled=True)]
  transfers between devices with their start and end apart: 3 -> 0, of which waited for: 2 -> 0; matrix products, arithmetic and copies ran while one was open for 0% -> 0% of each run, Pallas kernels for 0% -> 0%
where the time goes in v2:
time: 314 us; the launch traced here: 313 us
  Pallas kernels  275 us (88%)
  local copies, waits for them, and re-layouts  18.5 us (6%)
  between operations  14.6 us (5%)
  other arithmetic  4.48 us (1%)
    pallas_call x1, Pallas kernels, fused_path(): pl.pallas_call(functools.partial(fused_kernel, n_dev, n_row_dev, n_heads,...  275 us
    unnamed x1, local copies, waits for them, and re-layouts  10.5 us

profile of v2, /device:TPU:97, one launch (start us, length us, event | category | flops | bytes accessed | tf_op | source)
XLA Modules:
  0.0 312.9 jit_solution(17977750381295074015)
XLA Ops:
  6.5 0.7 abs_add_fusion
  7.2 0.8 multiply_reduce_fusion.2
  8.0 0.6 reduce_max.9
  8.6 0.9 multiply_reduce_fusion
  9.5 0.6 multiply_reduce_fusion.3
  11.3 284.3 %conditional.1 = (bf16[256,128,128]{2,1,0:T(8,128)(2,1)}) conditional(s32[]{:T(128)} %convert_element_type.26, (bf16[256,128,128]{2,1,0:T(8,128)(2,1)}, s32[1024]{0:T(1024)}, f32[128]{0:T(128)}, f32[128]{0:T(128)}, bf16[128,4]{0,1:T(4,128)(2,1)}, /*index=5*/bf16[128,128]{1,0:T(8,128)(2,1)}, bf16[128,128]{1,0:T(8,128)(2,1)}, ...), branch_computations={%region_5.6_spmd, %region_6.7_spmd} | conditional | flops 589862 | bytes 81558872 | solution.py:428
  11.5 0.8 dynamic-slice_bitcast_fusion
  12.3 1.3 pad.6.w_b_ref
  13.5 0.9 copy.29
  14.4 0.9 copy.28
  15.3 0.9 copy.27
  16.2 0.7 maximum_bitcast_fusion.1.w_qvg_ref
  16.8 0.9 copy.26
  17.8 0.6 copy.35
  18.4 0.7 copy.21.mask_ref
  19.1 0.3 broadcast_multiply_fusion
  19.4 0.1 copy.34
  19.5 1.0 copy.22.w_k_ref
  20.5 275.1 %branch_1_fun.1 = bf16[256,128,128]{2,1,0:T(8,128)(2,1)} custom-call(bf16[256,128,128]{2,1,0:T(8,128)(2,1)} %get-tuple-element.58.z_hbm, s32[128,1]{1,0:T(8,128)} %copy.21.mask_ref, f32[1,128]{1,0:T(1,128)} %bitcast.41, f32[1,128]{1,0:T(1,128)} %bitcast.38, bf16[8,128]{1,0:T(8,128)(2,1)} %pad.6.w_b_ref, bf16[512,512]{1,0:T(8,128)(2,1)} %copy.22.w_k_ref, ...), custom_call_target="tpu_custom_call" | custom-call | tf_op jit(solution)/shard_map/cond/branch_1_fun/pallas_call | solution.py:352
  295.6 10.5 %copy.39 = bf16[256,128,128]{2,1,0:T(8,128)(2,1)} copy(bf16[256,128,128]{2,1,0:T(8,128)(2,1)} %get-tuple-element.68) | data formatting | bytes 16777216
  (3 shorter events, 0.1 us)

commit v3 on v2

--- a/solution.py
+++ b/solution.py
@@ -41,7 +41,7 @@
             out_ref[head] = acc_ref[head].T.astype(jnp.bfloat16)
 
 
-def attend_kernel(z_ref, mask_ref, bias_ref, gamma_ref, beta_ref, w_k_ref, w_qvg_ref, w_o_ref, out_ref, bias_f32, q_scr, gate_scr):
+def attend_kernel(z_ref, mask_ref, bias_ref, gamma_ref, beta_ref, w_k_ref, w_qvg_ref, out_ref, bias_f32, q_scr, gate_scr):
     n_src, _, n_cols, pair_dim = z_ref.shape
     n_heads, n_keys, n_query = bias_ref.shape
     head_dim = pair_dim // n_heads
@@ -77,10 +77,8 @@
             attended = jnp.dot(v_all[rows], weights.astype(jnp.bfloat16), preferred_element_type=jnp.float32)
             gated.append((gate_scr[rows, pl.ds(jb, J_BLOCK)] * (attended / total)).astype(jnp.bfloat16))
         u_cols = jnp.concatenate(gated, axis=0)
-        update = lax.dot_general(u_cols, w_o_ref[...], (((0,), (0,)), ((), ())), preferred_element_type=jnp.float32)
-        n_blk = J_BLOCK // n_cols
-        z_blk = z_ref[pl.ds(blk_idx * n_blk, n_blk)].reshape(J_BLOCK, pair_dim).astype(jnp.float32)
-        out_ref[pl.ds(blk_idx * n_blk, n_blk)] = (z_blk + update).astype(jnp.bfloat16).reshape(n_blk, 1, n_cols, pair_dim)
+        for part in range(J_BLOCK // n_cols):
+            out_ref[blk_idx * (J_BLOCK // n_cols) + part, 0] = u_cols[:, part * n_cols : (part + 1) * n_cols]
         return 0
 
     lax.fori_loop(0, n_query // J_BLOCK, one_block, 0)
@@ -98,9 +96,9 @@
 
 def fused_kernel(
     n_dev, n_row_dev, n_heads, n_used,
-    z_hbm, mask_ref, gamma_ref, beta_ref, w_b_ref, w_k_ref, w_qvg_ref, w_o_ref, eye_ref,
+    z_hbm, mask_ref, gamma_ref, beta_ref, w_b_ref, w_k_ref, w_qvg_ref, eye_ref,
     out_hbm,
-    z_in, b_acc, b_all, z_rows, a_scr, k_scr, q_scr, v_scr, g_scr, s_scr, u_scr, o_scr,
+    z_in, b_acc, b_all, z_rows, a_scr, k_scr, q_scr, v_scr, g_scr, s_scr, o_scr,
     in_sem, own_sem, z_send, z_recv, bx_send, bx_recv, by_send, by_recv, bd_send, bd_recv, o_send, o_recv, o_own,
 ):
     me, row = lax.axis_index("col"), lax.axis_index("row")
@@ -160,7 +158,6 @@
     own_rows = pltpu.make_async_copy(z_hbm.at[pl.ds(me * rows_own, rows_own)], z_rows.at[me], own_sem)
     own_rows.start()
     start_z(0)
-    start_z(1)
 
     def load_chunk(idx):
         return pltpu.make_async_copy(z_hbm.at[pl.ds(idx * chunk, chunk)], z_in.at[lax.rem(idx, 2)], in_sem.at[lax.rem(idx, 2)])
@@ -184,8 +181,8 @@
     own_cols = pl.ds(pl.multiple_of(me * n_cols, n_cols), n_cols)
     for blk in range(blk_rows):
         for head in range(n_heads):
-            tile = b_acc[head, blk * n_cols : (blk + 1) * n_cols, :].T
-            b_all[row * blk_rows + blk, head, own_cols, :] = jnp.where(mask_ref[...] > 0, tile, MASK_NEG).astype(jnp.bfloat16)
+            tile = jnp.where(mask_ref[pl.ds(me, 1), :] > 0, b_acc[head, blk * n_cols : (blk + 1) * n_cols, :], MASK_NEG)
+            b_all[row * blk_rows + blk, head, own_cols, :] = tile.T.astype(jnp.bfloat16)
 
     def clear(idx, _):
         q_scr[idx] = jnp.zeros(q_scr.shape[1:], q_scr.dtype)
@@ -198,7 +195,7 @@
     for e in range(1, n_row_dev):
         by(0, e, row).start()
     bd(0, 0, me).start()
-    for step in range(2, n_steps):
+    for step in range(1, n_steps):
         start_z(step)
     for t in range(1, n_chip):
         bx(t, col_at(-2 * t)).wait_recv()
@@ -206,9 +203,11 @@
             by(t, e, row).start()
         bd(t, 0, me).start()
 
-    def prologue(step):
+    def wait_z(step):
         for d in range(1, n_dev):
             z_copy(step, d, me, col_at(-d)).wait_recv()
+
+    def prologue(step):
         for r in range(STEP_ROWS):
             normed = normalize(z_rows[:, step * STEP_ROWS + r].reshape(n_dev * n_cols, pair_dim), gamma_ref[...], beta_ref[...])
             a_scr[r] = normed
@@ -243,14 +242,6 @@
         new_top = fold8(scaled, jnp.max)
         return new_top if top is None else jnp.maximum(top, new_top)
 
-    def update_unit(step, unit):
-        jb, pair = lax.div(unit, 2), lax.rem(unit, 2)
-        update = lax.dot_general(u_scr[pair], w_o_ref[...], (((0,), (0,)), ((), ())), preferred_element_type=jnp.float32)
-        for half in range(2):
-            r = pair * 2 + half
-            z_blk = z_rows[jb, step * STEP_ROWS + r].astype(jnp.float32)
-            o_scr[lax.rem(step, 2), jb, r] = (z_blk + update[half * n_cols : (half + 1) * n_cols]).astype(jnp.bfloat16)
-
     def attend(step):
         def one_unit(unit, top):
             pair = lax.rem(unit, 2)
@@ -268,19 +259,19 @@
                     attended = prod if attended is None else attended + prod
                 inv = 1.0 / jnp.sum(total, axis=0, keepdims=True)
                 picked = jnp.concatenate([attended[:head_dim, :n_cols], attended[head_dim:, n_cols:]], axis=1)
-                u_scr[pair, head * head_dim : (head + 1) * head_dim, :] = (g_scr[unit, head] * (picked * inv)).astype(jnp.bfloat16)
+                gated = (g_scr[unit, head] * (picked * inv)).astype(jnp.bfloat16)
+                for half in range(2):
+                    o_scr[lax.rem(step, 2), lax.div(unit, 2), pair * 2 + half, head * head_dim : (head + 1) * head_dim, :] = gated[:, half * n_cols : (half + 1) * n_cols]
                 top = top_next
-                if head == 0:
-                    update_unit(step, jnp.maximum(unit - 1, 0))
             return top
 
         top = None
         for k0, kn in key_blocks:
             top = logits_of(0, 0, 0, k0, kn, top)
         lax.fori_loop(0, n_units, one_unit, top)
-        update_unit(step, n_units - 1)
 
     own_rows.wait()
+    wait_z(0)
     prologue(0)
     for t in range(n_chip):
         for e in range(1, n_row_dev):
@@ -299,6 +290,7 @@
 
         @pl.when(step >= 1)
         def _():
+            wait_z(step)
             prologue(step)
 
         attend(step)
@@ -330,30 +322,24 @@
     lax.fori_loop(0, n_steps, drain, 0)
 
 
-def fused_path(mesh, z_tile, res_mask, ln_gamma, ln_beta, w_q, w_k, w_v, w_g, w_b, w_o):
+def fused_path(mesh, z_tile, res_mask, gamma, beta, w_b_t, w_k, w_k_wide, w_qvg_t, eye):
     n_dev, n_row_dev = mesh.shape["col"], mesh.shape["row"]
     n_rows_loc, n_cols, pair_dim = z_tile.shape
-    n_heads = w_b.shape[1]
-    n_query = res_mask.shape[0]
+    n_heads = w_b_t.shape[0]
+    n_query = res_mask.size
     n_used = -(-(n_query - n_query // 5) // 64) * 64
     rows_own = n_rows_loc // n_dev
     n_steps = rows_own // STEP_ROWS
     head_dim = pair_dim // n_heads
-    mask_own = lax.dynamic_slice_in_dim(res_mask, lax.axis_index("col") * n_cols, n_cols)[:, None]
-    w_b_t = jnp.pad(w_b.T, ((0, 8 - n_heads), (0, 0)))
-    w_qvg_t = jnp.concatenate([w_q, w_v, w_g], axis=1).T
-    spread = jnp.eye(STEP_ROWS, dtype=w_k.dtype)
-    w_k_wide = jnp.einsum("rs,chd->rchsd", spread, w_k.reshape(pair_dim, n_heads, head_dim)).reshape(STEP_ROWS * pair_dim, n_heads * pair_dim)
-    eye = jnp.tile(jnp.eye(n_cols, dtype=jnp.bfloat16), (1, 2))
     whole = pl.BlockSpec(memory_space=pltpu.VMEM)
     hbm = pl.BlockSpec(memory_space=pl.ANY)
     bf16, f32, dma = jnp.bfloat16, jnp.float32, pltpu.SemaphoreType.DMA
     n_units = n_dev * 2
     return pl.pallas_call(
         functools.partial(fused_kernel, n_dev, n_row_dev, n_heads, n_used),
-        in_specs=[hbm] + [whole] * 8,
+        in_specs=[hbm] + [whole] * 7,
         out_specs=hbm,
-        out_shape=jax.ShapeDtypeStruct(z_tile.shape, bf16),
+        out_shape=jax.ShapeDtypeStruct((n_rows_loc, pair_dim, n_cols), bf16),
         scratch_shapes=[
             pltpu.VMEM((2, 16, n_cols, pair_dim), bf16),
             pltpu.VMEM((n_heads, n_rows_loc, n_cols), f32),
@@ -365,14 +351,45 @@
             pltpu.VMEM((2, n_heads, 2 * head_dim, n_query), bf16),
             pltpu.VMEM((n_units, n_heads, head_dim, 2 * n_cols), f32),
             pltpu.VMEM((2, n_used, 2 * n_cols), f32),
-            pltpu.VMEM((2, pair_dim, 2 * n_cols), bf16),
-            pltpu.VMEM((2, n_dev, STEP_ROWS, n_cols, pair_dim), bf16),
+            pltpu.VMEM((2, n_dev, STEP_ROWS, pair_dim, n_cols), bf16),
             dma((2,)), dma, dma((n_steps, n_dev)), dma((n_steps, n_dev)),
             dma((n_dev // 2,)), dma((n_dev // 2,)), dma((n_dev // 2, n_row_dev)), dma((n_dev // 2, n_row_dev)),
             dma((n_dev // 2, n_row_dev)), dma((n_dev // 2, n_row_dev)), dma((2, n_dev)), dma((n_steps, n_dev)), dma((2,)),
         ],
         compiler_params=pltpu.CompilerParams(collective_id=0, has_side_effects=True, vmem_limit_bytes=VMEM_LIMIT),
-    )(z_tile, mask_own, ln_gamma[None, :], ln_beta[None, :], w_b_t, w_k_wide, w_qvg_t, w_o, eye)
+    )(z_tile, res_mask, gamma, beta, w_b_t, w_k_wide, w_qvg_t, eye)
+
+
+def prepare_kernel(gamma_ref, beta_ref, w_q_ref, w_k_ref, w_v_ref, w_g_ref, w_b_ref, w_b_t_ref, w_k_wide_ref, w_qvg_t_ref, eye_ref, bound_ref):
+    n_heads, pair_dim = w_b_t_ref.shape
+    head_dim = pair_dim // n_heads
+    n_cols = eye_ref.shape[0]
+    bf16, f32 = jnp.bfloat16, jnp.float32
+    ones = lambda n, m, offset: (lax.broadcasted_iota(jnp.int32, (n, m), 0) + offset == lax.broadcasted_iota(jnp.int32, (n, m), 1)).astype(bf16)
+    eye_ref[...] = jnp.concatenate([ones(n_cols, n_cols, 0)] * 2, axis=1)
+    w_b_t_ref[...] = lax.dot_general(w_b_ref[...], ones(pair_dim, pair_dim, 0), (((0,), (0,)), ((), ())), preferred_element_type=f32).astype(bf16)
+    for idx, ref in enumerate((w_q_ref, w_v_ref, w_g_ref)):
+        w_qvg_t_ref[idx * pair_dim : (idx + 1) * pair_dim, :] = ref[...].astype(f32).T.astype(bf16)
+    w_k = w_k_ref[...].astype(f32)
+    lane_group = lax.div(lax.broadcasted_iota(jnp.int32, (pair_dim, pair_dim), 1), head_dim)
+    for r in range(STEP_ROWS):
+        for head in range(n_heads):
+            shift = (r - head) * head_dim % pair_dim
+            moved = pltpu.roll(w_k, shift, 1) if shift else w_k
+            w_k_wide_ref[r * pair_dim : (r + 1) * pair_dim, head * pair_dim : (head + 1) * pair_dim] = jnp.where(lane_group == r, moved, 0.0).astype(bf16)
+    largest = (pair_dim ** 0.5 * jnp.abs(gamma_ref[...]) + jnp.abs(beta_ref[...])).T
+    bound = lambda ref: jnp.sum(largest * jnp.abs(ref[...].astype(f32)), axis=0, keepdims=True)
+    bound_ref[...] = jnp.sum(bound(w_q_ref) * bound(w_k_ref), axis=1, keepdims=True) + jnp.max(bound(w_b_ref), axis=1, keepdims=True)
+
+
+def output_kernel(z_ref, u_ref, w_o_ref, out_ref):
+    for r in range(z_ref.shape[0]):
+        update = lax.dot_general(u_ref[r], w_o_ref[...], (((0,), (0,)), ((), ())), preferred_element_type=jnp.float32)
+        out_ref[r] = (z_ref[r].astype(jnp.float32) + update).astype(jnp.bfloat16)
+
+
+def spread_all(values, axis, size):
+    return lax.all_to_all(jnp.broadcast_to(values[None], (size,) + values.shape), axis, 0, 0, tiled=True)
 
 
 def solution(mesh):
@@ -381,13 +398,11 @@
     replicated = P()
     whole = pl.BlockSpec(memory_space=pltpu.VMEM)
 
-    def whole_keys_path(z_tile, res_mask, ln_gamma, ln_beta, w_q, w_k, w_v, w_g, w_b, w_o):
+    def whole_keys_path(z_tile, res_mask, gamma, beta, w_b_t, w_k, _, w_qvg_t, __):
         n_rows_loc, n_cols, pair_dim = z_tile.shape
-        n_heads = w_b.shape[1]
+        n_heads = w_b_t.shape[0]
         rows_own = n_rows_loc // n_col_dev
-        n_query = res_mask.shape[0]
-        gamma, beta = ln_gamma[None, :], ln_beta[None, :]
-        w_b_t = jnp.pad(w_b.T, ((0, 8 - n_heads), (0, 0)))
+        n_query = res_mask.size
         rows_step = 16
         bias_t = pl.pallas_call(
             bias_kernel,
@@ -398,34 +413,56 @@
             scratch_shapes=[pltpu.VMEM((n_heads, n_rows_loc, n_cols), jnp.float32)],
             compiler_params=pltpu.CompilerParams(vmem_limit_bytes=VMEM_LIMIT),
         )(z_tile, gamma, beta, w_b_t)
-        bias_t = lax.all_gather(bias_t, "col", axis=1, tiled=True)
-        bias_t = lax.all_gather(bias_t, "row", axis=2, tiled=True)
+        bias_t = spread_all(bias_t, "col", n_col_dev).transpose(1, 0, 2, 3).reshape(n_heads, n_query, n_rows_loc)
+        bias_t = spread_all(bias_t, "row", mesh.shape["row"]).transpose(1, 2, 0, 3).reshape(n_heads, n_query, n_query)
         z_own = lax.all_to_all(z_tile.reshape(n_col_dev, rows_own, n_cols, pair_dim), "col", 0, 0, tiled=True)
-        w_qvg_t = jnp.concatenate([w_q, w_v, w_g], axis=1).T
         blk = pl.BlockSpec((n_col_dev, 1, n_cols, pair_dim), lambda i: (0, i, 0, 0))
-        out = pl.pallas_call(
+        u_blk = pl.BlockSpec((n_col_dev, 1, pair_dim, n_cols), lambda i: (0, i, 0, 0))
+        u_own = pl.pallas_call(
             attend_kernel,
             grid=(rows_own,),
-            in_specs=[blk, whole, whole, whole, whole, whole, whole, whole],
-            out_specs=blk,
-            out_shape=jax.ShapeDtypeStruct(z_own.shape, jnp.bfloat16),
+            in_specs=[blk, whole, whole, whole, whole, whole, whole],
+            out_specs=u_blk,
+            out_shape=jax.ShapeDtypeStruct((n_col_dev, rows_own, pair_dim, n_cols), jnp.bfloat16),
             scratch_shapes=[
                 pltpu.VMEM((n_heads, n_query, n_query), jnp.float32),
                 pltpu.VMEM((n_heads, pair_dim, n_query), jnp.bfloat16),
                 pltpu.VMEM((pair_dim, n_query), jnp.float32),
             ],
             compiler_params=pltpu.CompilerParams(vmem_limit_bytes=VMEM_LIMIT),
-        )(z_own, res_mask[:, None], bias_t, gamma, beta, w_k, w_qvg_t, w_o)
-        out = lax.all_to_all(out, "col", 0, 0, tiled=True)
-        return out.reshape(n_rows_loc, n_cols, pair_dim)
-
-    def local_fn(*args):
-        _, _, ln_gamma, ln_beta, w_q, w_k, _, _, w_b, _ = args
-        pair_dim, n_heads = w_b.shape
-        largest = (pair_dim ** 0.5 * jnp.abs(ln_gamma) + jnp.abs(ln_beta))[:, None]
-        bound = lambda weight: jnp.sum(largest * jnp.abs(weight.astype(jnp.float32)), axis=0)
-        logit_bound = jnp.sum(bound(w_q) * bound(w_k)) + jnp.max(bound(w_b))
-        return lax.cond(logit_bound < 1e8, functools.partial(fused_path, mesh), whole_keys_path, *args)
+        )(z_own, res_mask.reshape(n_query, 1), bias_t, gamma, beta, w_k, w_qvg_t)
+        return lax.all_to_all(u_own, "col", 0, 0, tiled=True).reshape(n_rows_loc, pair_dim, n_cols)
+
+    def local_fn(z_tile, res_mask, ln_gamma, ln_beta, w_q, w_k, w_v, w_g, w_b, w_o):
+        n_rows_loc, n_cols, pair_dim = z_tile.shape
+        n_heads = w_b.shape[1]
+        gamma, beta = ln_gamma[None, :], ln_beta[None, :]
+        bf16 = jnp.bfloat16
+        w_b_t, w_k_wide, w_qvg_t, eye, logit_bound = pl.pallas_call(
+            prepare_kernel,
+            in_specs=[whole] * 7,
+            out_specs=[whole] * 5,
+            out_shape=[
+                jax.ShapeDtypeStruct((n_heads, pair_dim), bf16),
+                jax.ShapeDtypeStruct((STEP_ROWS * pair_dim, n_heads * pair_dim), bf16),
+                jax.ShapeDtypeStruct((3 * pair_dim, pair_dim), bf16),
+                jax.ShapeDtypeStruct((n_cols, 2 * n_cols), bf16),
+                jax.ShapeDtypeStruct((1, 1), jnp.float32),
+            ],
+        )(gamma, beta, w_q, w_k, w_v, w_g, w_b)
+        u_tile = lax.cond(
+            logit_bound[0, 0] < 1e8, functools.partial(fused_path, mesh), whole_keys_path,
+            z_tile, res_mask.reshape(-1, n_cols), gamma, beta, w_b_t, w_k, w_k_wide, w_qvg_t, eye)
+        rows_step = 16
+        z_blk = pl.BlockSpec((rows_step, n_cols, pair_dim), lambda i: (i, 0, 0))
+        return pl.pallas_call(
+            output_kernel,
+            grid=(n_rows_loc // rows_step,),
+            in_specs=[z_blk, pl.BlockSpec((rows_step, pair_dim, n_cols), lambda i: (i, 0, 0)), whole],
+            out_specs=z_blk,
+            out_shape=jax.ShapeDtypeStruct(z_tile.shape, bf16),
+            compiler_params=pltpu.CompilerParams(vmem_limit_bytes=VMEM_LIMIT),
+        )(z_tile, u_tile, w_o)
 
     return jax.shard_map(
         local_fn,

time: 314 us -> 274 us (0.87)
  local copies, waits for them, and re-layouts: 18.5 us -> 1.41 us
  between operations: 14.6 us -> 0.64 us
  other arithmetic: 4.48 us -> 0 us
  Pallas kernels: 275 us -> 271 us
    pallas_call x1, Pallas kernels: 275 us -> 254 us  [fused_path(): pl.pallas_call(functools.partial(fused_kernel, n_dev, n_row_dev, n_heads,...]
    pallas_call x0 -> x2, Pallas kernels: none -> 17.5 us  [the longest x1 15.7 us: local_fn(): pl.pallas_call(output_kernel, grid=(n_rows_loc // rows_step,), in_specs=[...]
    unnamed x1, local copies, waits for them, and re-layouts: 10.5 us -> 1.41 us
    another operation x5 -> x0, local copies, waits for them, and re-layouts: 3.5 us -> none
where the time goes in v3:
time: 274 us
  Pallas kernels  271 us (99%)
    pallas_call x1, Pallas kernels, fused_path(): pl.pallas_call(functools.partial(fused_kernel, n_dev, n_row_dev, n_heads,...  254 us
    pallas_call x1, Pallas kernels, local_fn(): pl.pallas_call(output_kernel, grid=(n_rows_loc // rows_step,), in_specs=[...  15.7 us

profile of v3, /device:TPU:97, one launch (start us, length us, event | category | flops | bytes accessed | tf_op | source)
XLA Modules:
  0.0 273.6 jit_solution(16245972669207216463)
XLA Ops:
  0.0 1.4 copy.20.w_b_ref
  1.4 1.7 shard_map.100
  3.8 254.1 %conditional.1 = (bf16[256,128,128]{2,1,0:T(8,128)(2,1)}) conditional(s32[]{:T(128)} %bitcast.10, (bf16[256,128,128]{2,1,0:T(8,128)(2,1)}, s32[1024]{0:T(1024)}, f32[1,128]{1,0:T(1,128)}, f32[1,128]{1,0:T(1,128)}, bf16[4,128]{1,0:T(4,128)(2,1)S(1)}, /*index=5*/bf16[128,128]{1,0:T(8,128)(2,1)}, bf16[384,128]{1,0:T(8,128)(2,1)S(1)}) %tuple.17, ...), branch_computations={%region_0.0_spmd, %region_1.0_spmd} | conditional | bytes 96891040 | solution.py:453
  4.0 253.9 %branch_1_fun.1 = bf16[256,128,128]{2,1,0:T(8,128)(2,1)} custom-call(bf16[256,128,128]{2,1,0:T(8,128)(2,1)} %get-tuple-element.45.z_hbm, s32[8,128]{1,0:T(8,128)} %bitcast.19, f32[1,128]{1,0:T(1,128)} %get-tuple-element.47.gamma_ref, f32[1,128]{1,0:T(1,128)} %get-tuple-element.48.beta_ref, bf16[4,128]{1,0:T(4,128)(2,1)S(1)} %get-tuple-element.49.w_b_ref, ...), custom_call_target="tpu_custom_call" | custom-call | tf_op jit(solution)/shard_map/cond/branch_1_fun/pallas_call | solution.py:338
  257.9 15.7 %shard_map.101 = bf16[256,128,128]{2,1,0:T(8,128)(2,1)} custom-call(bf16[256,128,128]{2,1,0:T(8,128)(2,1)} %z_ref.1, bf16[256,128,128]{2,1,0:T(8,128)(2,1)} %get-tuple-element.64.u_ref, bf16[128,128]{1,0:T(8,128)(2,1)} %w_o_ref.1), custom_call_target="tpu_custom_call" | custom-call | tf_op jit(solution)/shard_map/pallas_call | solution.py:458

commit v4 on v3

--- a/solution.py
+++ b/solution.py
@@ -87,7 +87,7 @@
 MESH = pl.DeviceIdType.MESH
 LOG2E = 1.4426950408889634
 STEP_ROWS = 4
-KEY_CHUNK = 416
+KEY_CHUNK = 208
 
 
 def fold8(values, op):
@@ -185,29 +185,37 @@
             b_all[row * blk_rows + blk, head, own_cols, :] = tile.T.astype(jnp.bfloat16)
 
     def clear(idx, _):
-        q_scr[idx] = jnp.zeros(q_scr.shape[1:], q_scr.dtype)
+        for slot in range(2):
+            q_scr[slot, idx] = jnp.zeros(q_scr.shape[2:], q_scr.dtype)
         return 0
 
-    lax.fori_loop(0, q_scr.shape[0], clear, 0)
-
-    for d in range(1, n_chip):
-        bx(d, me).start()
-    for e in range(1, n_row_dev):
-        by(0, e, row).start()
-    bd(0, 0, me).start()
+    lax.fori_loop(0, q_scr.shape[1], clear, 0)
+
+    used = lambda col: col * n_cols < n_used
+
+    def forward(t, offsets):
+        @pl.when(used(col_at(-2 * t)))
+        def _():
+            for e in offsets:
+                by(t, e, row).start()
+            bd(t, 0, me).start()
+
+    @pl.when(used(me))
+    def _():
+        for d in range(1, n_chip):
+            bx(d, me).start()
+
+    row_order = [1, 3, 2]
+    forward(0, row_order)
     for step in range(1, n_steps):
         start_z(step)
-    for t in range(1, n_chip):
-        bx(t, col_at(-2 * t)).wait_recv()
-        for e in range(1, n_row_dev):
-            by(t, e, row).start()
-        bd(t, 0, me).start()
 
     def wait_z(step):
         for d in range(1, n_dev):
             z_copy(step, d, me, col_at(-d)).wait_recv()
 
     def prologue(step):
+        slot = lax.rem(step, 2)
         for r in range(STEP_ROWS):
             normed = normalize(z_rows[:, step * STEP_ROWS + r].reshape(n_dev * n_cols, pair_dim), gamma_ref[...], beta_ref[...])
             a_scr[r] = normed
@@ -218,68 +226,105 @@
             gate = jax.nn.sigmoid(qvg[2 * pair_dim :])
             for head in range(n_heads):
                 hs = slice(head * head_dim, (head + 1) * head_dim)
-                v_scr[pair, head, half * head_dim : (half + 1) * head_dim, :] = v_all[hs]
+                v_scr[slot, pair, head, half * head_dim : (half + 1) * head_dim, :] = v_all[hs]
                 for jb in range(n_dev):
                     js = slice(jb * n_cols, (jb + 1) * n_cols)
                     ls = slice(half * n_cols, (half + 1) * n_cols)
-                    q_scr[jb * 2 + pair, head, r * head_dim : (r + 1) * head_dim, ls] = q_all[hs, js]
-                    g_scr[jb * 2 + pair, head, :, ls] = gate[hs, js]
+                    q_scr[slot, jb * 2 + pair, head, r * head_dim : (r + 1) * head_dim, ls] = q_all[hs, js]
+                    g_scr[slot, jb * 2 + pair, head, :, ls] = gate[hs, js]
         for k0 in range(0, n_used, 128):
             kn = min(128, n_used - k0)
             a_cat = jnp.concatenate([a_scr[r, k0 : k0 + kn, :] for r in range(STEP_ROWS)], axis=1)
             k_all = jnp.dot(a_cat, w_k_ref[...], preferred_element_type=jnp.float32).astype(jnp.bfloat16)
             for head in range(n_heads):
-                k_scr[head, k0 : k0 + kn, :] = k_all[:, head * pair_dim : (head + 1) * pair_dim]
+                k_scr[slot, head, k0 : k0 + kn, :] = k_all[:, head * pair_dim : (head + 1) * pair_dim]
 
     key_blocks = [(k0, min(KEY_CHUNK, n_used - k0)) for k0 in range(0, n_used, KEY_CHUNK)]
     n_units = n_dev * 2
-
-    def logits_of(head, unit, slot, k0, kn, top):
-        lhs = jnp.concatenate([k_scr[head, k0 : k0 + kn, :], b_all[lax.div(unit, 2), head, k0 : k0 + kn, :]], axis=1)
-        rhs = jnp.concatenate([q_scr[unit, head], eye_ref[...]], axis=0)
+    row_units = n_units // n_row_dev
+
+    def offset_of(turn):
+        return turn + lax.div(turn, 2) - 2 * lax.div(turn, 3)
+
+    def unit_at(turn_unit):
+        return row_at(-offset_of(lax.div(turn_unit, row_units))) * row_units + lax.rem(turn_unit, row_units)
+
+    def wait_bias(turn):
+        e = offset_of(turn)
+        for t in range(n_chip):
+            @pl.when(used(col_at(-2 * t)))
+            def _():
+                by(t, e, row_at(-e)).wait_recv()
+                bd(t, e, me).start()
+
+        for t in range(n_chip):
+            @pl.when(used(lax.rem(partner - 2 * t + n_dev, n_dev)))
+            def _():
+                bd(t, e, partner).wait_recv()
+
+    def logits_of(slot, head, unit, buf, k0, kn, top):
+        lhs = jnp.concatenate([k_scr[slot, head, k0 : k0 + kn, :], b_all[lax.div(unit, 2), head, k0 : k0 + kn, :]], axis=1)
+        rhs = jnp.concatenate([q_scr[slot, unit, head], eye_ref[...]], axis=0)
         scaled = jnp.dot(lhs, rhs, preferred_element_type=jnp.float32) * LOG2E
-        s_scr[slot, k0 : k0 + kn, :] = scaled
+        s_scr[buf, k0 : k0 + kn, :] = scaled
         new_top = fold8(scaled, jnp.max)
         return new_top if top is None else jnp.maximum(top, new_top)
 
     def attend(step):
-        def one_unit(unit, top):
+        slot, out_slot = lax.rem(step, 2), lax.rem(step, 2)
+
+        def one_unit(turn_unit, top):
+            last_of_row = lax.rem(turn_unit, row_units) == row_units - 1
+
+            @pl.when((turn_unit == row_units - 1) & (step + 1 < n_steps))
+            def _():
+                wait_z(step + 1)
+                prologue(step + 1)
+
+            @pl.when((step == 0) & last_of_row & (turn_unit < n_units - 1))
+            def _():
+                wait_bias(lax.div(turn_unit, row_units) + 1)
+
+            unit, unit_next = unit_at(turn_unit), unit_at(jnp.minimum(turn_unit + 1, n_units - 1))
             pair = lax.rem(unit, 2)
-            unit_next = jnp.minimum(unit + 1, n_units - 1)
             for head in range(n_heads):
                 head_next, from_unit = (head + 1, unit) if head + 1 < n_heads else (0, unit_next)
                 top_row = jnp.max(top, axis=0, keepdims=True)
                 top_next = total = attended = None
                 for k0, kn in key_blocks:
-                    top_next = logits_of(head_next, from_unit, (head + 1) % 2, k0, kn, top_next)
+                    top_next = logits_of(slot, head_next, from_unit, (head + 1) % 2, k0, kn, top_next)
+                for k0, kn in key_blocks:
                     weights = jnp.exp2(s_scr[head % 2, k0 : k0 + kn, :] - top_row)
                     part = fold8(weights, jnp.sum)
                     total = part if total is None else total + part
-                    prod = jnp.dot(v_scr[pair, head, :, k0 : k0 + kn], weights.astype(jnp.bfloat16), preferred_element_type=jnp.float32)
+                    prod = jnp.dot(v_scr[slot, pair, head, :, k0 : k0 + kn], weights.astype(jnp.bfloat16), preferred_element_type=jnp.float32)
                     attended = prod if attended is None else attended + prod
                 inv = 1.0 / jnp.sum(total, axis=0, keepdims=True)
                 picked = jnp.concatenate([attended[:head_dim, :n_cols], attended[head_dim:, n_cols:]], axis=1)
-                gated = (g_scr[unit, head] * (picked * inv)).astype(jnp.bfloat16)
+                gated = (g_scr[slot, unit, head] * (picked * inv)).astype(jnp.bfloat16)
                 for half in range(2):
-                    o_scr[lax.rem(step, 2), lax.div(unit, 2), pair * 2 + half, head * head_dim : (head + 1) * head_dim, :] = gated[:, half * n_cols : (half + 1) * n_cols]
+                    o_scr[out_slot, lax.div(unit, 2), pair * 2 + half, head * head_dim : (head + 1) * head_dim, :] = gated[:, half * n_cols : (half + 1) * n_cols]
                 top = top_next
             return top
 
         top = None
         for k0, kn in key_blocks:
-            top = logits_of(0, 0, 0, k0, kn, top)
+            top = logits_of(slot, 0, unit_at(0), 0, k0, kn, top)
         lax.fori_loop(0, n_units, one_unit, top)
 
     own_rows.wait()
     wait_z(0)
     prologue(0)
+    for t in range(1, n_chip):
+        @pl.when(used(col_at(-2 * t)))
+        def _():
+            bx(t, col_at(-2 * t)).wait_recv()
+
+        forward(t, row_order)
     for t in range(n_chip):
-        for e in range(1, n_row_dev):
-            by(t, e, row_at(-e)).wait_recv()
-            bd(t, e, me).start()
-    for t in range(n_chip):
-        for e in range(n_row_dev):
-            bd(t, e, partner).wait_recv()
+        @pl.when(used(lax.rem(partner - 2 * t + n_dev, n_dev)))
+        def _():
+            bd(t, 0, partner).wait_recv()
 
     def one_step(step, _):
         @pl.when(step >= 2)
@@ -288,11 +333,6 @@
                 out_copy(step - 2, d, col_at(d), me).wait_send()
             out_own(step - 2).wait()
 
-        @pl.when(step >= 1)
-        def _():
-            wait_z(step)
-            prologue(step)
-
         attend(step)
         for d in range(1, n_dev):
             out_copy(step, d, col_at(d), me).start()
@@ -305,13 +345,18 @@
         for d in range(1, n_dev):
             out_copy(step, d, col_at(d), me).wait_send()
         out_own(step).wait()
-    for d in range(1, n_chip):
-        bx(d, me).wait_send()
+    @pl.when(used(me))
+    def _():
+        for d in range(1, n_chip):
+            bx(d, me).wait_send()
+
     for t in range(n_chip):
-        for e in range(1, n_row_dev):
-            by(t, e, row).wait_send()
-        for e in range(n_row_dev):
-            bd(t, e, me).wait_send()
+        @pl.when(used(col_at(-2 * t)))
+        def _():
+            for e in range(1, n_row_dev):
+                by(t, e, row).wait_send()
+            for e in range(n_row_dev):
+                bd(t, e, me).wait_send()
 
     def drain(step, _):
         for d in range(1, n_dev):
@@ -346,10 +391,10 @@
             pltpu.VMEM((n_query // n_cols, n_heads, n_query, n_cols), bf16),
             pltpu.VMEM((n_dev, rows_own, n_cols, pair_dim), bf16),
             pltpu.VMEM((STEP_ROWS, n_query, pair_dim), bf16),
-            pltpu.VMEM((n_heads, n_query, STEP_ROWS * head_dim), bf16),
-            pltpu.VMEM((n_units, n_heads, STEP_ROWS * head_dim, 2 * n_cols), bf16),
-            pltpu.VMEM((2, n_heads, 2 * head_dim, n_query), bf16),
-            pltpu.VMEM((n_units, n_heads, head_dim, 2 * n_cols), f32),
+            pltpu.VMEM((2, n_heads, n_query, STEP_ROWS * head_dim), bf16),
+            pltpu.VMEM((2, n_units, n_heads, STEP_ROWS * head_dim, 2 * n_cols), bf16),
+            pltpu.VMEM((2, 2, n_heads, 2 * head_dim, n_query), bf16),
+            pltpu.VMEM((2, n_units, n_heads, head_dim, 2 * n_cols), f32),
             pltpu.VMEM((2, n_used, 2 * n_cols), f32),
             pltpu.VMEM((2, n_dev, STEP_ROWS, pair_dim, n_cols), bf16),
             dma((2,)), dma, dma((n_steps, n_dev)), dma((n_steps, n_dev)),

time: 274 us -> 273 us (level)
  no operation moved by 1% of the time
where the time goes in v4:
time: 273 us
  Pallas kernels  270 us (99%)
    pallas_call x1, Pallas kernels, fused_path(): pl.pallas_call(functools.partial(fused_kernel, n_dev, n_row_dev, n_heads,...  253 us
    pallas_call x1, Pallas kernels, local_fn(): pl.pallas_call(output_kernel, grid=(n_rows_loc // rows_step,), in_specs=[...  15.7 us

profile of v4, /device:TPU:97, one launch (start us, length us, event | category | flops | bytes accessed | tf_op | source)
XLA Modules:
  0.0 272.5 jit_solution(15902761946584231597)
XLA Ops:
  0.0 1.4 copy.20.w_b_ref
  1.4 1.7 shard_map.100
  3.8 253.0 %conditional.1 = (bf16[256,128,128]{2,1,0:T(8,128)(2,1)}) conditional(s32[]{:T(128)} %bitcast.10, (bf16[256,128,128]{2,1,0:T(8,128)(2,1)}, s32[1024]{0:T(1024)}, f32[1,128]{1,0:T(1,128)}, f32[1,128]{1,0:T(1,128)}, bf16[4,128]{1,0:T(4,128)(2,1)S(1)}, /*index=5*/bf16[128,128]{1,0:T(8,128)(2,1)}, bf16[384,128]{1,0:T(8,128)(2,1)S(1)}) %tuple.17, ...), branch_computations={%region_0.0_spmd, %region_1.0_spmd} | conditional | bytes 96891040 | solution.py:498
  3.8 252.8 %branch_1_fun.1 = bf16[256,128,128]{2,1,0:T(8,128)(2,1)} custom-call(bf16[256,128,128]{2,1,0:T(8,128)(2,1)} %get-tuple-element.45.z_hbm, s32[8,128]{1,0:T(8,128)} %bitcast.19, f32[1,128]{1,0:T(1,128)} %get-tuple-element.47.gamma_ref, f32[1,128]{1,0:T(1,128)} %get-tuple-element.48.beta_ref, bf16[4,128]{1,0:T(4,128)(2,1)S(1)} %get-tuple-element.49.w_b_ref, ...), custom_call_target="tpu_custom_call" | custom-call | tf_op jit(solution)/shard_map/cond/branch_1_fun/pallas_call | solution.py:383
  256.8 15.7 %shard_map.101 = bf16[256,128,128]{2,1,0:T(8,128)(2,1)} custom-call(bf16[256,128,128]{2,1,0:T(8,128)(2,1)} %z_ref.1, bf16[256,128,128]{2,1,0:T(8,128)(2,1)} %get-tuple-element.64.u_ref, bf16[128,128]{1,0:T(8,128)(2,1)} %w_o_ref.1), custom_call_target="tpu_custom_call" | custom-call | tf_op jit(solution)/shard_map/pallas_call | solution.py:503

commit v5 on v4

--- a/solution.py
+++ b/solution.py
@@ -148,12 +148,21 @@
 
     def out_copy(step, d, to, at):
         return pltpu.make_async_remote_copy(
-            o_scr.at[lax.rem(step, 2), to], out_hbm.at[pl.ds(at * rows_own + step * STEP_ROWS, STEP_ROWS)],
-            o_send.at[lax.rem(step, 2), d], o_recv.at[step, d], device_id={"col": to}, device_id_type=MESH)
+            o_scr.at[step, to], out_hbm.at[pl.ds(at * rows_own + step * STEP_ROWS, STEP_ROWS)],
+            o_send.at[step, d], o_recv.at[step, d], device_id={"col": to}, device_id_type=MESH)
 
     def out_own(step):
         return pltpu.make_async_copy(
-            o_scr.at[lax.rem(step, 2), me], out_hbm.at[pl.ds(me * rows_own + step * STEP_ROWS, STEP_ROWS)], o_own.at[lax.rem(step, 2)])
+            o_scr.at[step, me], out_hbm.at[pl.ds(me * rows_own + step * STEP_ROWS, STEP_ROWS)], o_own.at[step])
+
+    def send_out(step, to):
+        @pl.when(to == me)
+        def _():
+            out_own(step).start()
+
+        @pl.when(to != me)
+        def _():
+            out_copy(step, lax.rem(to - me + n_dev, n_dev), to, me).start()
 
     own_rows = pltpu.make_async_copy(z_hbm.at[pl.ds(me * rows_own, rows_own)], z_rows.at[me], own_sem)
     own_rows.start()
@@ -184,12 +193,11 @@
             tile = jnp.where(mask_ref[pl.ds(me, 1), :] > 0, b_acc[head, blk * n_cols : (blk + 1) * n_cols, :], MASK_NEG)
             b_all[row * blk_rows + blk, head, own_cols, :] = tile.T.astype(jnp.bfloat16)
 
-    def clear(idx, _):
-        for slot in range(2):
-            q_scr[slot, idx] = jnp.zeros(q_scr.shape[2:], q_scr.dtype)
+    def clear(slot, idx, _):
+        q_scr[slot, idx] = jnp.zeros(q_scr.shape[2:], q_scr.dtype)
         return 0
 
-    lax.fori_loop(0, q_scr.shape[1], clear, 0)
+    lax.fori_loop(0, q_scr.shape[1], functools.partial(clear, 0), 0)
 
     used = lambda col: col * n_cols < n_used
 
@@ -271,7 +279,7 @@
         return new_top if top is None else jnp.maximum(top, new_top)
 
     def attend(step):
-        slot, out_slot = lax.rem(step, 2), lax.rem(step, 2)
+        slot = lax.rem(step, 2)
 
         def one_unit(turn_unit, top):
             last_of_row = lax.rem(turn_unit, row_units) == row_units - 1
@@ -280,6 +288,10 @@
             def _():
                 wait_z(step + 1)
                 prologue(step + 1)
+
+            @pl.when((lax.rem(turn_unit, 2) == 1) & (turn_unit >= 3))
+            def _():
+                send_out(step, lax.div(unit_at(jnp.maximum(turn_unit - 2, 0)), 2))
 
             @pl.when((step == 0) & last_of_row & (turn_unit < n_units - 1))
             def _():
@@ -303,7 +315,7 @@
                 picked = jnp.concatenate([attended[:head_dim, :n_cols], attended[head_dim:, n_cols:]], axis=1)
                 gated = (g_scr[slot, unit, head] * (picked * inv)).astype(jnp.bfloat16)
                 for half in range(2):
-                    o_scr[out_slot, lax.div(unit, 2), pair * 2 + half, head * head_dim : (head + 1) * head_dim, :] = gated[:, half * n_cols : (half + 1) * n_cols]
+                    o_scr[step, lax.div(unit, 2), pair * 2 + half, head * head_dim : (head + 1) * head_dim, :] = gated[:, half * n_cols : (half + 1) * n_cols]
                 top = top_next
             return top
 
@@ -312,6 +324,7 @@
             top = logits_of(slot, 0, unit_at(0), 0, k0, kn, top)
         lax.fori_loop(0, n_units, one_unit, top)
 
+    lax.fori_loop(0, q_scr.shape[1], functools.partial(clear, 1), 0)
     own_rows.wait()
     wait_z(0)
     prologue(0)
@@ -327,24 +340,12 @@
             bd(t, 0, partner).wait_recv()
 
     def one_step(step, _):
-        @pl.when(step >= 2)
-        def _():
-            for d in range(1, n_dev):
-                out_copy(step - 2, d, col_at(d), me).wait_send()
-            out_own(step - 2).wait()
-
         attend(step)
-        for d in range(1, n_dev):
-            out_copy(step, d, col_at(d), me).start()
-        out_own(step).start()
+        send_out(step, lax.div(unit_at(n_units - 1), 2))
         return 0
 
     lax.fori_loop(0, n_steps, one_step, 0)
 
-    for step in range(n_steps - 2, n_steps):
-        for d in range(1, n_dev):
-            out_copy(step, d, col_at(d), me).wait_send()
-        out_own(step).wait()
     @pl.when(used(me))
     def _():
         for d in range(1, n_chip):
@@ -361,7 +362,9 @@
     def drain(step, _):
         for d in range(1, n_dev):
             z_copy(step, d, col_at(d), me).wait_send()
+            out_copy(step, d, col_at(d), me).wait_send()
             out_copy(step, d, me, col_at(-d)).wait_recv()
+        out_own(step).wait()
         return 0
 
     lax.fori_loop(0, n_steps, drain, 0)
@@ -396,10 +399,10 @@
             pltpu.VMEM((2, 2, n_heads, 2 * head_dim, n_query), bf16),
             pltpu.VMEM((2, n_units, n_heads, head_dim, 2 * n_cols), f32),
             pltpu.VMEM((2, n_used, 2 * n_cols), f32),
-            pltpu.VMEM((2, n_dev, STEP_ROWS, pair_dim, n_cols), bf16),
+            pltpu.VMEM((n_steps, n_dev, STEP_ROWS, pair_dim, n_cols), bf16),
             dma((2,)), dma, dma((n_steps, n_dev)), dma((n_steps, n_dev)),
             dma((n_dev // 2,)), dma((n_dev // 2,)), dma((n_dev // 2, n_row_dev)), dma((n_dev // 2, n_row_dev)),
-            dma((n_dev // 2, n_row_dev)), dma((n_dev // 2, n_row_dev)), dma((2, n_dev)), dma((n_steps, n_dev)), dma((2,)),
+            dma((n_dev // 2, n_row_dev)), dma((n_dev // 2, n_row_dev)), dma((n_steps, n_dev)), dma((n_steps, n_dev)), dma((n_steps,)),
         ],
         compiler_params=pltpu.CompilerParams(collective_id=0, has_side_effects=True, vmem_limit_bytes=VMEM_LIMIT),
     )(z_tile, res_mask, gamma, beta, w_b_t, w_k_wide, w_qvg_t, eye)
@@ -498,7 +501,7 @@
         u_tile = lax.cond(
             logit_bound[0, 0] < 1e8, functools.partial(fused_path, mesh), whole_keys_path,
             z_tile, res_mask.reshape(-1, n_cols), gamma, beta, w_b_t, w_k, w_k_wide, w_qvg_t, eye)
-        rows_step = 16
+        rows_step = 64
         z_blk = pl.BlockSpec((rows_step, n_cols, pair_dim), lambda i: (i, 0, 0))
         return pl.pallas_call(
             output_kernel,

time: 273 us -> 245 us (0.90)
  Pallas kernels: 270 us -> 241 us
    pallas_call x1, Pallas kernels: 253 us -> 230 us  [fused_path(): pl.pallas_call(functools.partial(fused_kernel, n_dev, n_row_dev, n_heads,...]
    pallas_call x1, Pallas kernels: 15.7 us -> 10.1 us  [local_fn(): pl.pallas_call(output_kernel, grid=(n_rows_loc // rows_step,), in_specs=[...]
where the time goes in v5:
time: 245 us; the launch traced here: 244 us
  Pallas kernels  241 us (98%)
    pallas_call x1, Pallas kernels, fused_path(): pl.pallas_call(functools.partial(fused_kernel, n_dev, n_row_dev, n_heads,...  230 us
    pallas_call x1, Pallas kernels, local_fn(): pl.pallas_call(output_kernel, grid=(n_rows_loc // rows_step,), in_specs=[...  10.1 us

profile of v5, /device:TPU:97, one launch (start us, length us, event | category | flops | bytes accessed | tf_op | source)
XLA Modules:
  0.0 243.6 jit_solution(10228331361830008386)
XLA Ops:
  0.0 1.4 copy.20.w_b_ref
  1.4 1.7 shard_map.100
  3.8 229.8 %conditional.1 = (bf16[256,128,128]{2,1,0:T(8,128)(2,1)}) conditional(s32[]{:T(128)} %bitcast.10, (bf16[256,128,128]{2,1,0:T(8,128)(2,1)}, s32[1024]{0:T(1024)}, f32[1,128]{1,0:T(1,128)}, f32[1,128]{1,0:T(1,128)}, bf16[4,128]{1,0:T(4,128)(2,1)S(1)}, /*index=5*/bf16[128,128]{1,0:T(8,128)(2,1)}, bf16[384,128]{1,0:T(8,128)(2,1)S(1)}) %tuple.17, ...), branch_computations={%region_0.0_spmd, %region_1.0_spmd} | conditional | bytes 96891040 | solution.py:501
  3.8 229.5 %branch_1_fun.1 = bf16[256,128,128]{2,1,0:T(8,128)(2,1)} custom-call(bf16[256,128,128]{2,1,0:T(8,128)(2,1)} %get-tuple-element.45.z_hbm, s32[8,128]{1,0:T(8,128)} %bitcast.19, f32[1,128]{1,0:T(1,128)} %get-tuple-element.47.gamma_ref, f32[1,128]{1,0:T(1,128)} %get-tuple-element.48.beta_ref, bf16[4,128]{1,0:T(4,128)(2,1)S(1)} %get-tuple-element.49.w_b_ref, ...), custom_call_target="tpu_custom_call" | custom-call | tf_op jit(solution)/shard_map/cond/branch_1_fun/pallas_call | solution.py:386
  233.5 10.1 %shard_map.101 = bf16[256,128,128]{2,1,0:T(8,128)(2,1)} custom-call(bf16[256,128,128]{2,1,0:T(8,128)(2,1)} %z_ref.1, bf16[256,128,128]{2,1,0:T(8,128)(2,1)} %get-tuple-element.64.u_ref, bf16[128,128]{1,0:T(8,128)(2,1)} %w_o_ref.1), custom_call_target="tpu_custom_call" | custom-call | tf_op jit(solution)/shard_map/pallas_call | solution.py:506
